TPU v7x, 128 devices: a whole 4x4x4 slice. The times are simulated.
128 devices in a mesh: gx: 8 (over z, x_lo), gy: 16 (over y, x_hi, core).
Axes of the slice: x: 4 (x_hi: 2, x_lo: 2; x = x_hi * 2 + x_lo), y: 4, z: 4, core: 2. Of those that a mesh axis runs over, the one named last changes fastest.
Arguments:
- probes: float32 [8, 128, 256, 512], P(None, 'gx', 'gy'), may hold values from -12.5 to 12.5, as said below
- disorder: float32 [128, 256, 512], P('gx', 'gy'), may hold values from -2 to 2
- spectrum_center: float32 [1], replicated, may hold values from -0.5 to 0.5
- half_width: float32 [1], replicated, may hold values from 9 to 11
Outputs:
- last_vector: float32 [8, 128, 256, 512], P(None, 'gx', 'gy')
- moments: float32 [8, 8], replicated
Inputs may be any that keep to these rules, and one draw needn't show every extreme that they name: `probes`: real-valued probe entries.
All inputs are finite; a program needn't handle non-finite values.
Results may differ from a plain program's by a relative error of at most 0.0001.
Values sent between devices are 32-bit elements; how exact they have to be, the bound alone decides.
A program may use at most 128 MiB of HBM per device.

v0:
```python
import functools

import jax
import jax.numpy as jnp
from jax import lax
from jax.sharding import Mesh
from jax.sharding import PartitionSpec as P

STEPS = 4
GX_GY = ("gx_0", "gx_1", "gy_0", "gy_1", "gy_2")
GX = ("gx_0", "gx_1")
GY = ("gy_0", "gy_1", "gy_2")


def over_axes(array, axes):
    return functools.reduce(lax.psum, axes, array)


def extended(block, sides, width):
    for axis, dim in sides:
        count = lax.axis_size(axis)
        forward = [(i, i + 1) for i in range(count - 1)]
        forward.append((count - 1, 0))
        backward = [(target, source) for source, target in forward]
        low = lax.ppermute(
            lax.slice_in_dim(block, block.shape[dim] - width, None, axis=dim), axis, forward
        )
        high = lax.ppermute(lax.slice_in_dim(block, 0, width, axis=dim), axis, backward)
        block = jnp.concatenate([low, block, high], axis=dim)
    return block


def scaled_apply(ext, eps_part, center, width):
    core = ext[:, 1:-1, 1:-1]
    beside = ext[:, 2:, 1:-1] + ext[:, :-2, 1:-1] + ext[:, 1:-1, 2:] + ext[:, 1:-1, :-2]
    beside = beside + jnp.roll(core, 1, 3) + jnp.roll(core, -1, 3)
    return ((eps_part - center) * core - beside) / width


def inner_pair(t_low, t_high):
    square = jnp.sum(t_low * t_low, axis=(1, 2, 3))
    cross = jnp.sum(t_high * t_low, axis=(1, 2, 3))
    return jnp.stack([square, cross])


def settle(pair):
    return over_axes(pair, GX_GY)


def with_rim(field):
    return extended(field, ((GX, 1), (GY, 2)), 1)


def local(probes, disorder, spectrum_center, half_width):
    center = spectrum_center[0]
    width = half_width[0]
    energy = disorder[None]
    collected = []

    def keep(pair):
        collected.append(settle(pair))

    t_low = probes
    t_high = scaled_apply(with_rim(t_low), energy, center, width)
    for step in range(STEPS):
        keep(inner_pair(t_low, t_high))
        if step + 1 < STEPS:
            t_next = 2.0 * scaled_apply(with_rim(t_high), energy, center, width) - t_low
            t_low, t_high = (t_high, t_next)
    stacked = jnp.stack(collected)
    total_sites = (
        probes.shape[1] * lax.axis_size(GX) * probes.shape[2] * lax.axis_size(GY) * probes.shape[3]
    )
    sites = jnp.float32(total_sites)
    square = stacked[:, 0, :] / sites
    cross = stacked[:, 1, :] / sites
    even = 2.0 * square - square[0]
    odd = 2.0 * cross - cross[0]
    moments = jnp.stack([even, odd], axis=1).reshape(2 * STEPS, -1).T
    return (t_high, moments)


def solution(mesh):
    split = Mesh(mesh.devices.reshape(4, 2, 4, 2, 2), ("gx_0", "gx_1", "gy_0", "gy_1", "gy_2"))
    in_specs = (P(None, GX, GY, None), P(GX, GY, None), P(), P())
    out_specs = (P(None, GX, GY, None), P())
    return jax.shard_map(local, mesh=split, in_specs=in_specs, out_specs=out_specs, check_vma=False)
```

profile of v0, /device:TPU:1, one launch (start us, length us, event | category | flops | bytes accessed | tf_op | source)
XLA Modules:
  0.0 195.6 jit_solution(11918763609849999228)
XLA Ops:
  0.6 5.4 %copy.7 = f32[8,16,16,512]{3,0,2,1:T(8,128)S(1)} copy(f32[8,16,16,512]{3,2,1,0:T(8,128)} %param.4) | data formatting | bytes 8388608 | tf_op args[0]
  6.1 2.1 %collective-permute-start.1 = (f32[8,1,16,512]{3,0,2,1:T(8,128)S(1)}, f32[8,1,16,512]{3,0,2,1:T(8,128)S(1)}, u32[]{:S(2)}, u32[]{:S(2)}) collective-permute-start(f32[8,1,16,512]{3,0,2,1:T(8,128)S(1)} %get-tuple-element.65), channel_id=1, source_target_pairs={{0,16},{16,32},{32,48},{48,64},{64,80},{80,96},{96,112},{112,0},{1... | collective-permute-start | bytes 786440 | tf_op jit(solution)/shard_map/ppermute | solution.py:25
  8.2 3.6 %collective-permute-start = (f32[8,1,16,512]{3,0,2,1:T(8,128)S(1)}, f32[8,1,16,512]{3,0,2,1:T(8,128)S(1)}, u32[]{:S(2)}, u32[]{:S(2)}) collective-permute-start(f32[8,1,16,512]{3,0,2,1:T(8,128)S(1)} %get-tuple-element.64), channel_id=1, source_target_pairs={{16,0},{32,16},{48,32},{64,48},{80,64},{96,80},{112,96},{0,112},{1... | collective-permute-start | bytes 786440 | tf_op jit(solution)/shard_map/ppermute | solution.py:28
  11.8 3.5 %fusion.47 = (f32[8,16,16,511]{3,0,2,1:T(8,128)S(1)}, f32[8,16,16,511]{3,0,2,1:T(8,128)}) fusion(f32[8,16,16,512]{3,0,2,1:T(8,128)S(1)} %copy.7), kind=kLoop, calls=%fused_computation.108 | loop fusion | bytes 16744448 | tf_op jit(solution)/shard_map/jit(_roll_static)/slice | solution.py:36
  16.7 0.5 multiply_reduce_fusion.7
  17.1 0.6 collective-permute-done.1
  17.7 3.3 %constant_dynamic-update-slice_fusion.1 = f32[8,18,16,512]{3,0,2,1:T(8,128)S(1)} fusion(f32[8,18,16,512]{3,0,2,1:T(8,128)S(1)} %constant_dynamic-update-slice_fusion.2, f32[8,16,16,512]{3,2,1,0:T(8,128)S(1)} %copy-done.1), kind=kLoop, calls=%fused_computation.81 | loop fusion | bytes 8388608
  21.3 2.0 %collective-permute-start.2 = (f32[8,18,1,512]{3,0,2,1:T(8,128)S(1)}, f32[8,18,1,512]{3,0,2,1:T(8,128)S(1)}, u32[]{:S(2)}, u32[]{:S(2)}) collective-permute-start(f32[8,18,1,512]{3,0,2,1:T(8,128)S(1)} %get-tuple-element.40), channel_id=1, source_target_pairs={{1,0},{2,1},{3,2},{4,3},{5,4},{6,5},{7,6},{8,7},{9,8},{10,9},{11,1... | collective-permute-start | bytes 884744 | tf_op jit(solution)/shard_map/ppermute | solution.py:28
  23.3 2.9 %collective-permute-start.3 = (f32[8,18,1,512]{3,0,2,1:T(8,128)S(1)}, f32[8,18,1,512]{3,0,2,1:T(8,128)S(1)}, u32[]{:S(2)}, u32[]{:S(2)}) collective-permute-start(f32[8,18,1,512]{3,0,2,1:T(8,128)S(1)} %get-tuple-element.41), channel_id=1, source_target_pairs={{0,1},{1,2},{2,3},{3,4},{4,5},{5,6},{6,7},{7,8},{8,9},{9,10},{10,1... | collective-permute-start | bytes 884744 | tf_op jit(solution)/shard_map/ppermute | solution.py:25
  26.1 0.4 fusion.48
  26.5 4.3 %collective-permute-done.2 = f32[8,18,1,512]{3,0,2,1:T(8,128)S(1)} collective-permute-done((f32[8,18,1,512]{3,0,2,1:T(8,128)S(1)}, f32[8,18,1,512]{3,0,2,1:T(8,128)S(1)}, u32[]{:S(2)}, u32[]{:S(2)}) %collective-permute-start.2) | collective-permute-done | bytes 294944 | tf_op jit(solution)/shard_map/ppermute | solution.py:28
  30.8 1.2 collective-permute-done.3
  32.0 0.7 copy-done.11
  32.7 8.1 %fusion.31 = f32[8,16,16,512]{3,0,2,1:T(8,128)S(1)} fusion(f32[8,18,16,512]{3,0,2,1:T(8,128)} %copy-done.3, f32[8,18,1,512]{3,0,2,1:T(8,128)} %copy-done.11, f32[8,18,1,512]{3,0,2,1:T(8,128)} %copy-done.8, f32[8,16,16,512]{3,0,2,1:T(8,128)S(1)} %copy.7, f32[8,1,16,512]{3,0,2,1:T(8,128)S(1)} %collective-permute-done.1, f32[8,1,16,512]{3,0,2,1:T(8,128)} %copy-done.4, ...), kind=kLoop, calls=%fused_computation.56 | loop fusion | flops 14680064 | bytes 23134212 | tf_op jit(solution)/shard_map/div | solution.py:37
  40.8 1.3 collective-permute-start.4
  42.1 0.3 collective-permute-start.5
  42.4 4.9 %fusion.44 = (f32[8,16,16,511]{3,0,2,1:T(8,128)}, f32[8,16,16,511]{3,0,2,1:T(8,128)}) fusion(f32[8,16,16,512]{3,0,2,1:T(8,128)S(1)} %fusion.31), kind=kLoop, calls=%fused_computation.105 | loop fusion | bytes 16744448 | tf_op jit(solution)/shard_map/jit(_roll_static)/slice | solution.py:36
  47.2 3.5 %collective-permute-done.5 = f32[8,1,16,512]{3,0,2,1:T(8,128)S(1)} collective-permute-done((f32[8,1,16,512]{3,0,2,1:T(8,128)S(1)}, f32[8,1,16,512]{3,0,2,1:T(8,128)S(1)}, u32[]{:S(2)}, u32[]{:S(2)}) %collective-permute-start.5) | collective-permute-done | bytes 262176 | tf_op jit(solution)/shard_map/ppermute | solution.py:25
  50.8 6.2 %collective-permute-start.6 = (f32[8,18,1,512]{3,0,2,1:T(8,128)S(1)}, f32[8,18,1,512]{3,0,2,1:T(8,128)S(1)}, u32[]{:S(2)}, u32[]{:S(2)}) collective-permute-start(f32[8,18,1,512]{3,0,2,1:T(8,128)S(1)} %get-tuple-element.38), channel_id=1, source_target_pairs={{1,0},{2,1},{3,2},{4,3},{5,4},{6,5},{7,6},{8,7},{9,8},{10,9},{11,1... | collective-permute-start | bytes 884744 | tf_op jit(solution)/shard_map/ppermute | solution.py:28
  57.0 3.1 %collective-permute-start.7 = (f32[8,18,1,512]{3,0,2,1:T(8,128)S(1)}, f32[8,18,1,512]{3,0,2,1:T(8,128)S(1)}, u32[]{:S(2)}, u32[]{:S(2)}) collective-permute-start(f32[8,18,1,512]{3,0,2,1:T(8,128)S(1)} %get-tuple-element.39), channel_id=1, source_target_pairs={{0,1},{1,2},{2,3},{3,4},{4,5},{5,6},{6,7},{7,8},{8,9},{9,10},{10,1... | collective-permute-start | bytes 884744 | tf_op jit(solution)/shard_map/ppermute | solution.py:25
  60.1 0.4 fusion.45
  60.5 4.9 %collective-permute-done.6 = f32[8,18,1,512]{3,0,2,1:T(8,128)S(1)} collective-permute-done((f32[8,18,1,512]{3,0,2,1:T(8,128)S(1)}, f32[8,18,1,512]{3,0,2,1:T(8,128)S(1)}, u32[]{:S(2)}, u32[]{:S(2)}) %collective-permute-start.6) | collective-permute-done | bytes 294944 | tf_op jit(solution)/shard_map/ppermute | solution.py:28
  65.4 0.7 copy-done.9
  66.2 12.0 %fusion.24 = f32[8,16,16,512]{3,0,2,1:T(8,128)S(1)} fusion(f32[8,18,1,512]{3,0,2,1:T(8,128)} %copy-done.12, f32[8,1,16,512]{3,0,2,1:T(8,128)S(1)} %collective-permute-done.4, f32[8,16,16,512]{3,0,2,1:T(8,128)S(1)} %fusion.31, f32[8,1,16,512]{3,0,2,1:T(8,128)} %copy-done.5, f32[8,18,1,512]{3,0,2,1:T(8,128)} %copy-done.9, ...), kind=kLoop, calls=%fused_computation.41 | loop fusion | flops 20971520 | bytes 22609924 | tf_op jit(solution)/shard_map/sub | solution.py:68
  78.3 1.6 collective-permute-start.8
  79.9 4.9 %fusion.41 = (f32[8,16,16,511]{3,0,2,1:T(8,128)}, f32[8,16,16,511]{3,0,2,1:T(8,128)}) fusion(f32[8,16,16,512]{3,0,2,1:T(8,128)S(1)} %fusion.24), kind=kLoop, calls=%fused_computation.102 | loop fusion | bytes 16744448 | tf_op jit(solution)/shard_map/jit(_roll_static)/slice | solution.py:36
  84.8 2.8 %collective-permute-done.9 = f32[8,1,16,512]{3,0,2,1:T(8,128)S(1)} collective-permute-done((f32[8,1,16,512]{3,0,2,1:T(8,128)S(1)}, f32[8,1,16,512]{3,0,2,1:T(8,128)S(1)}, u32[]{:S(2)}, u32[]{:S(2)}) %collective-permute-start.9) | collective-permute-done | bytes 262176 | tf_op jit(solution)/shard_map/ppermute | solution.py:25
  87.7 9.0 %collective-permute-start.10 = (f32[8,18,1,512]{3,0,2,1:T(8,128)S(1)}, f32[8,18,1,512]{3,0,2,1:T(8,128)S(1)}, u32[]{:S(2)}, u32[]{:S(2)}) collective-permute-start(f32[8,18,1,512]{3,0,2,1:T(8,128)S(1)} %get-tuple-element.36), channel_id=1, source_target_pairs={{1,0},{2,1},{3,2},{4,3},{5,4},{6,5},{7,6},{8,7},{9,8},{10,9},{11,1... | collective-permute-start | bytes 884744 | tf_op jit(solution)/shard_map/ppermute | solution.py:28
  96.6 0.4 fusion.42
  97.0 2.4 %collective-permute-done.10 = f32[8,18,1,512]{3,0,2,1:T(8,128)S(1)} collective-permute-done((f32[8,18,1,512]{3,0,2,1:T(8,128)S(1)}, f32[8,18,1,512]{3,0,2,1:T(8,128)S(1)}, u32[]{:S(2)}, u32[]{:S(2)}) %collective-permute-start.10) | collective-permute-done | bytes 294944 | tf_op jit(solution)/shard_map/ppermute | solution.py:28
  99.4 2.8 %collective-permute-done.11 = f32[8,18,1,512]{3,0,2,1:T(8,128)S(1)} collective-permute-done((f32[8,18,1,512]{3,0,2,1:T(8,128)S(1)}, f32[8,18,1,512]{3,0,2,1:T(8,128)S(1)}, u32[]{:S(2)}, u32[]{:S(2)}) %collective-permute-start.11) | collective-permute-done | bytes 294944 | tf_op jit(solution)/shard_map/ppermute | solution.py:25
  102.2 0.7 copy-done.13
  103.0 9.0 %fusion.15 = f32[8,16,16,512]{3,0,2,1:T(8,128)} fusion(f32[8,16,16,512]{3,0,2,1:T(8,128)S(1)} %fusion.31, f32[8,18,1,512]{3,0,2,1:T(8,128)} %copy-done.13, f32[8,1,16,512]{3,0,2,1:T(8,128)S(1)} %collective-permute-done.8, f32[8,16,16,512]{3,0,2,1:T(8,128)S(1)} %fusion.24, f32[8,1,16,512]{3,0,2,1:T(8,128)} %copy-done.6, f32[8,18,1,512]{3,0,2,1:T(8,128)} %copy-done.10, ...), kind=kLoop, calls=%fused_computation.24 | loop fusion | flops 20971520 | bytes 22609924 | tf_op jit(solution)/shard_map/sub | solution.py:68
  112.0 1.1 fusion.38
  113.2 1.3 collective-permute-start.13
  114.6 8.1 %fusion.40 = (f32[8,16,16,511]{3,0,2,1:T(8,128)}, f32[8,16,16,511]{3,0,2,1:T(8,128)}) fusion(f32[8,16,16,512]{3,0,2,1:T(8,128)} %fusion.15), kind=kLoop, calls=%fused_computation.101 | loop fusion | bytes 16744448 | tf_op jit(solution)/shard_map/jit(_roll_static)/slice | solution.py:36
  122.7 9.3 %collective-permute-start.14 = (f32[8,18,1,512]{3,0,2,1:T(8,128)S(1)}, f32[8,18,1,512]{3,0,2,1:T(8,128)S(1)}, u32[]{:S(2)}, u32[]{:S(2)}) collective-permute-start(f32[8,18,1,512]{3,0,2,1:T(8,128)S(1)} %get-tuple-element.34), channel_id=1, source_target_pairs={{1,0},{2,1},{3,2},{4,3},{5,4},{6,5},{7,6},{8,7},{9,8},{10,9},{11,1... | collective-permute-start | bytes 884744 | tf_op jit(solution)/shard_map/ppermute | solution.py:28
  132.1 0.4 fusion.39
  132.5 1.5 collective-permute-done.14
  133.9 2.1 %collective-permute-done.15 = f32[8,18,1,512]{3,0,2,1:T(8,128)S(1)} collective-permute-done((f32[8,18,1,512]{3,0,2,1:T(8,128)S(1)}, f32[8,18,1,512]{3,0,2,1:T(8,128)S(1)}, u32[]{:S(2)}, u32[]{:S(2)}) %collective-permute-start.15) | collective-permute-done | bytes 294944 | tf_op jit(solution)/shard_map/ppermute | solution.py:25
  136.0 13.2 %multiply_reduce_fusion.1 = (f32[8]{0:T(128)S(1)}, f32[8]{0:T(128)S(1)}, f32[8]{0:T(128)S(1)}, f32[8]{0:T(128)S(1)}, f32[8]{0:T(128)S(1)}, /*index=5*/f32[8]{0:T(128)S(1)}, f32[8]{0:T(128)S(1)}, f32[8,16,16,512]{3,0,2,1:T(8,128)}) fusion(f32[8,16,16,512]{3,0,2,1:T(8,128)S(1)} %copy-done, f32[8,16,16,512]{3,0,2,1:T(8,128)S(1)} %fusion.24, ...), kind=kLoop, calls=%fused_computation.63 | loop fusion | flops 35651528 | bytes 30998756 | tf_op jit(solution)/shard_map/reduce_sum | solution.py:41
  149.2 7.1 %all-reduce.1 = (f32[2,8]{1,0:T(2,128)S(1)}, f32[2,8]{1,0:T(2,128)S(1)}, f32[2,8]{1,0:T(2,128)S(1)}, f32[2,8]{1,0:T(2,128)S(1)}) all-reduce(f32[2,8]{1,0:T(2,128)S(1)} %get-tuple-element.70, f32[2,8]{1,0:T(2,128)S(1)} %get-tuple-element.71, ...), channel_id=1, replica_groups=mesh['gx_0'=4,'gx_1'=2,'gy_0'=4,'gy_1'=2,'gy_2'=2] {'gx_0'}, use_global_device_ids=true, to_apply=%region_2.3 | all-reduce | flops 64 | bytes 512 | tf_op jit(solution)/shard_map/psum | solution.py:16
  156.4 6.1 %all-reduce.4 = (f32[2,8]{1,0:T(2,128)S(1)}, f32[2,8]{1,0:T(2,128)S(1)}, f32[2,8]{1,0:T(2,128)S(1)}, f32[2,8]{1,0:T(2,128)S(1)}) all-reduce(f32[2,8]{1,0:T(2,128)S(1)} %get-tuple-element.17, f32[2,8]{1,0:T(2,128)S(1)} %get-tuple-element.18, ...), channel_id=1, replica_groups=mesh['gx_0'=4,'gx_1'=2,'gy_0'=4,'gy_1'=2,'gy_2'=2] {'gx_1'}, use_global_device_ids=true, to_apply=%region_3.4 | all-reduce | flops 64 | bytes 512 | tf_op jit(solution)/shard_map/psum | solution.py:16
  162.5 6.8 %all-reduce = (f32[2,8]{1,0:T(2,128)S(1)}, f32[2,8]{1,0:T(2,128)S(1)}, f32[2,8]{1,0:T(2,128)S(1)}, f32[2,8]{1,0:T(2,128)S(1)}) all-reduce(f32[2,8]{1,0:T(2,128)S(1)} %get-tuple-element.29, f32[2,8]{1,0:T(2,128)S(1)} %get-tuple-element.30, ...), channel_id=1, replica_groups=mesh['gx_0'=4,'gx_1'=2,'gy_0'=4,'gy_1'=2,'gy_2'=2] {'gy_0'}, use_global_device_ids=true, to_apply=%region_4.5 | all-reduce | flops 64 | bytes 512 | tf_op jit(solution)/shard_map/psum | solution.py:16
  169.2 8.4 %all-reduce.3 = (f32[2,8]{1,0:T(2,128)S(1)}, f32[2,8]{1,0:T(2,128)S(1)}, f32[2,8]{1,0:T(2,128)S(1)}, f32[2,8]{1,0:T(2,128)S(1)}) all-reduce(f32[2,8]{1,0:T(2,128)S(1)} %get-tuple-element.13, f32[2,8]{1,0:T(2,128)S(1)} %get-tuple-element.14, ...), channel_id=1, replica_groups=mesh['gx_0'=4,'gx_1'=2,'gy_0'=4,'gy_1'=2,'gy_2'=2] {'gy_1'}, use_global_device_ids=true, to_apply=%region_5.6 | all-reduce | flops 64 | bytes 512 | tf_op jit(solution)/shard_map/psum | solution.py:16
  177.6 10.6 %all-reduce.2 = (f32[1,2,8]{2,1,0:T(2,128)S(1)}, f32[1,2,8]{2,1,0:T(2,128)S(1)}, f32[1,2,8]{2,1,0:T(2,128)S(1)}, f32[1,2,8]{2,1,0:T(2,128)S(1)}) all-reduce(f32[1,2,8]{2,1,0:T(2,128)S(1)} %bitcast.35, f32[1,2,8]{2,1,0:T(2,128)S(1)} %bitcast.36, ...), channel_id=1, replica_groups=mesh['gx_0'=4,'gx_1'=2,'gy_0'=4,'gy_1'=2,'gy_2'=2] {'gy_2'}, use_global_device_ids=true, to_apply=%region_6.7 | all-reduce | flops 64 | bytes 512 | tf_op jit(solution)/shard_map/psum | solution.py:16
  188.4 0.7 copy.20
  189.0 6.6 %copy.19 = f32[8,16,16,512]{3,2,1,0:T(8,128)} copy(f32[8,16,16,512]{3,0,2,1:T(8,128)} %get-tuple-element.33) | data formatting | bytes 8388608
  (56 shorter events, 1.0 us)
Async XLA Ops:
  6.1 11.6 %collective-permute-start.1 = (f32[8,1,16,512]{3,0,2,1:T(8,128)S(1)}, f32[8,1,16,512]{3,0,2,1:T(8,128)S(1)}, u32[]{:S(2)}, u32[]{:S(2)}) collective-permute-start(f32[8,1,16,512]{3,0,2,1:T(8,128)S(1)} %get-tuple-element.65), channel_id=1, source_target_pairs={{0,16},{16,32},{32,48},{48,64},{64,80},{80,96},{96,112},{112,0},{1... | collective-permute-start | bytes 786440 | tf_op jit(solution)/shard_map/ppermute | solution.py:25
  8.2 8.4 %copy-start.7 = (f32[16,16,512]{2,1,0:T(8,128)S(1)}, f32[16,16,512]{2,1,0:T(8,128)}, u32[]{:S(2)}) copy-start(f32[16,16,512]{2,1,0:T(8,128)} %param.5) | copy-start | bytes 1572868
  8.2 8.4 %copy-start.1 = (f32[8,16,16,512]{3,2,1,0:T(8,128)S(1)}, f32[8,16,16,512]{3,2,1,0:T(8,128)}, u32[]{:S(2)}) copy-start(f32[8,16,16,512]{3,2,1,0:T(8,128)} %param.4) | copy-start | bytes 12582916
  8.2 12.9 %collective-permute-start = (f32[8,1,16,512]{3,0,2,1:T(8,128)S(1)}, f32[8,1,16,512]{3,0,2,1:T(8,128)S(1)}, u32[]{:S(2)}, u32[]{:S(2)}) collective-permute-start(f32[8,1,16,512]{3,0,2,1:T(8,128)S(1)} %get-tuple-element.64), channel_id=1, source_target_pairs={{16,0},{32,16},{48,32},{64,48},{80,64},{96,80},{112,96},{0,112},{1... | collective-permute-start | bytes 786440 | tf_op jit(solution)/shard_map/ppermute | solution.py:28
  21.2 2.1 %copy-start.4 = (f32[8,1,16,512]{3,0,2,1:T(8,128)}, f32[8,1,16,512]{3,0,2,1:T(8,128)S(1)}, u32[]{:S(2)}) copy-start(f32[8,1,16,512]{3,0,2,1:T(8,128)S(1)} %collective-permute-done) | copy-start | bytes 786436
  21.2 10.8 %copy-start.3 = (f32[8,18,16,512]{3,0,2,1:T(8,128)}, f32[8,18,16,512]{3,0,2,1:T(8,128)S(1)}, u32[]{:S(2)}) copy-start(f32[8,18,16,512]{3,0,2,1:T(8,128)S(1)} %constant_dynamic-update-slice_fusion) | copy-start | bytes 14155780
  21.3 9.6 %collective-permute-start.2 = (f32[8,18,1,512]{3,0,2,1:T(8,128)S(1)}, f32[8,18,1,512]{3,0,2,1:T(8,128)S(1)}, u32[]{:S(2)}, u32[]{:S(2)}) collective-permute-start(f32[8,18,1,512]{3,0,2,1:T(8,128)S(1)} %get-tuple-element.40), channel_id=1, source_target_pairs={{1,0},{2,1},{3,2},{4,3},{5,4},{6,5},{7,6},{8,7},{9,8},{10,9},{11,1... | collective-permute-start | bytes 884744 | tf_op jit(solution)/shard_map/ppermute | solution.py:28
  23.3 8.7 %collective-permute-start.3 = (f32[8,18,1,512]{3,0,2,1:T(8,128)S(1)}, f32[8,18,1,512]{3,0,2,1:T(8,128)S(1)}, u32[]{:S(2)}, u32[]{:S(2)}) collective-permute-start(f32[8,18,1,512]{3,0,2,1:T(8,128)S(1)} %get-tuple-element.41), channel_id=1, source_target_pairs={{0,1},{1,2},{2,3},{3,4},{4,5},{5,6},{6,7},{7,8},{8,9},{9,10},{10,1... | collective-permute-start | bytes 884744 | tf_op jit(solution)/shard_map/ppermute | solution.py:25
  30.8 1.2 copy-start.8
  32.0 0.7 copy-start.11
  40.8 6.4 %collective-permute-start.4 = (f32[8,1,16,512]{3,0,2,1:T(8,128)S(1)}, f32[8,1,16,512]{3,0,2,1:T(8,128)S(1)}, u32[]{:S(2)}, u32[]{:S(2)}) collective-permute-start(f32[8,1,16,512]{3,0,2,1:T(8,128)S(1)} %get-tuple-element.59), channel_id=1, source_target_pairs={{16,0},{32,16},{48,32},{64,48},{80,64},{96,80},{112,96},{0,112},{1... | collective-permute-start | bytes 786440 | tf_op jit(solution)/shard_map/ppermute | solution.py:28
  42.1 8.6 %collective-permute-start.5 = (f32[8,1,16,512]{3,0,2,1:T(8,128)S(1)}, f32[8,1,16,512]{3,0,2,1:T(8,128)S(1)}, u32[]{:S(2)}, u32[]{:S(2)}) collective-permute-start(f32[8,1,16,512]{3,0,2,1:T(8,128)S(1)} %get-tuple-element.58), channel_id=1, source_target_pairs={{0,16},{16,32},{32,48},{48,64},{64,80},{80,96},{96,112},{112,0},{1... | collective-permute-start | bytes 786440 | tf_op jit(solution)/shard_map/ppermute | solution.py:25
  50.8 6.2 %copy-start.5 = (f32[8,1,16,512]{3,0,2,1:T(8,128)}, f32[8,1,16,512]{3,0,2,1:T(8,128)S(1)}, u32[]{:S(2)}) copy-start(f32[8,1,16,512]{3,0,2,1:T(8,128)S(1)} %collective-permute-done.5) | copy-start | bytes 786436
  50.8 14.6 %collective-permute-start.6 = (f32[8,18,1,512]{3,0,2,1:T(8,128)S(1)}, f32[8,18,1,512]{3,0,2,1:T(8,128)S(1)}, u32[]{:S(2)}, u32[]{:S(2)}) collective-permute-start(f32[8,18,1,512]{3,0,2,1:T(8,128)S(1)} %get-tuple-element.38), channel_id=1, source_target_pairs={{1,0},{2,1},{3,2},{4,3},{5,4},{6,5},{7,6},{8,7},{9,8},{10,9},{11,1... | collective-permute-start | bytes 884744 | tf_op jit(solution)/shard_map/ppermute | solution.py:28
  57.0 8.4 %collective-permute-start.7 = (f32[8,18,1,512]{3,0,2,1:T(8,128)S(1)}, f32[8,18,1,512]{3,0,2,1:T(8,128)S(1)}, u32[]{:S(2)}, u32[]{:S(2)}) collective-permute-start(f32[8,18,1,512]{3,0,2,1:T(8,128)S(1)} %get-tuple-element.39), channel_id=1, source_target_pairs={{0,1},{1,2},{2,3},{3,4},{4,5},{5,6},{6,7},{7,8},{8,9},{9,10},{10,1... | collective-permute-start | bytes 884744 | tf_op jit(solution)/shard_map/ppermute | solution.py:25
  65.4 0.7 copy-start.9
  65.4 0.8 copy-start.12
  78.3 6.5 %collective-permute-start.8 = (f32[8,1,16,512]{3,0,2,1:T(8,128)S(1)}, f32[8,1,16,512]{3,0,2,1:T(8,128)S(1)}, u32[]{:S(2)}, u32[]{:S(2)}) collective-permute-start(f32[8,1,16,512]{3,0,2,1:T(8,128)S(1)} %get-tuple-element.53), channel_id=1, source_target_pairs={{16,0},{32,16},{48,32},{64,48},{80,64},{96,80},{112,96},{0,112},{1... | collective-permute-start | bytes 786440 | tf_op jit(solution)/shard_map/ppermute | solution.py:28
  79.9 7.7 %collective-permute-start.9 = (f32[8,1,16,512]{3,0,2,1:T(8,128)S(1)}, f32[8,1,16,512]{3,0,2,1:T(8,128)S(1)}, u32[]{:S(2)}, u32[]{:S(2)}) collective-permute-start(f32[8,1,16,512]{3,0,2,1:T(8,128)S(1)} %get-tuple-element.52), channel_id=1, source_target_pairs={{0,16},{16,32},{32,48},{48,64},{64,80},{80,96},{96,112},{112,0},{1... | collective-permute-start | bytes 786440 | tf_op jit(solution)/shard_map/ppermute | solution.py:25
  87.6 9.0 %copy-start.6 = (f32[8,1,16,512]{3,0,2,1:T(8,128)}, f32[8,1,16,512]{3,0,2,1:T(8,128)S(1)}, u32[]{:S(2)}) copy-start(f32[8,1,16,512]{3,0,2,1:T(8,128)S(1)} %collective-permute-done.9) | copy-start | bytes 786436
  87.7 11.8 %collective-permute-start.10 = (f32[8,18,1,512]{3,0,2,1:T(8,128)S(1)}, f32[8,18,1,512]{3,0,2,1:T(8,128)S(1)}, u32[]{:S(2)}, u32[]{:S(2)}) collective-permute-start(f32[8,18,1,512]{3,0,2,1:T(8,128)S(1)} %get-tuple-element.36), channel_id=1, source_target_pairs={{1,0},{2,1},{3,2},{4,3},{5,4},{6,5},{7,6},{8,7},{9,8},{10,9},{11,1... | collective-permute-start | bytes 884744 | tf_op jit(solution)/shard_map/ppermute | solution.py:28
  96.6 5.6 %collective-permute-start.11 = (f32[8,18,1,512]{3,0,2,1:T(8,128)S(1)}, f32[8,18,1,512]{3,0,2,1:T(8,128)S(1)}, u32[]{:S(2)}, u32[]{:S(2)}) collective-permute-start(f32[8,18,1,512]{3,0,2,1:T(8,128)S(1)} %get-tuple-element.37), channel_id=1, source_target_pairs={{0,1},{1,2},{2,3},{3,4},{4,5},{5,6},{6,7},{7,8},{8,9},{9,10},{10,1... | collective-permute-start | bytes 884744 | tf_op jit(solution)/shard_map/ppermute | solution.py:25
  99.4 2.8 %copy-start.10 = (f32[8,18,1,512]{3,0,2,1:T(8,128)}, f32[8,18,1,512]{3,0,2,1:T(8,128)S(1)}, u32[]{:S(2)}) copy-start(f32[8,18,1,512]{3,0,2,1:T(8,128)S(1)} %collective-permute-done.10) | copy-start | bytes 884740
  102.2 0.7 copy-start.13
  113.0 9.6 %collective-permute-start.12 = (f32[8,1,16,512]{3,0,2,1:T(8,128)S(1)}, f32[8,1,16,512]{3,0,2,1:T(8,128)S(1)}, u32[]{:S(2)}, u32[]{:S(2)}) collective-permute-start(f32[8,1,16,512]{3,0,2,1:T(8,128)S(1)} %get-tuple-element.43), channel_id=1, source_target_pairs={{16,0},{32,16},{48,32},{64,48},{80,64},{96,80},{112,96},{0,112},{1... | collective-permute-start | bytes 786440 | tf_op jit(solution)/shard_map/ppermute | solution.py:28
  113.2 9.4 %copy-start = (f32[8,16,16,512]{3,0,2,1:T(8,128)S(1)}, f32[8,16,16,512]{3,0,2,1:T(8,128)}, u32[]{:S(2)}) copy-start(f32[8,16,16,512]{3,0,2,1:T(8,128)} %fusion.15) | copy-start | bytes 12582916
  113.2 9.4 %collective-permute-start.13 = (f32[8,1,16,512]{3,0,2,1:T(8,128)S(1)}, f32[8,1,16,512]{3,0,2,1:T(8,128)S(1)}, u32[]{:S(2)}, u32[]{:S(2)}) collective-permute-start(f32[8,1,16,512]{3,0,2,1:T(8,128)S(1)} %get-tuple-element.42), channel_id=1, source_target_pairs={{0,16},{16,32},{32,48},{48,64},{64,80},{80,96},{96,112},{112,0},{1... | collective-permute-start | bytes 786440 | tf_op jit(solution)/shard_map/ppermute | solution.py:25
  122.7 13.4 %copy-start.2 = (f32[8,16,16,512]{3,2,1,0:T(8,128)S(1)}, f32[8,16,16,512]{3,2,1,0:T(8,128)}, u32[]{:S(2)}) copy-start(f32[8,16,16,512]{3,2,1,0:T(8,128)} %param.4) | copy-start | bytes 12582916
  122.7 11.2 %collective-permute-start.14 = (f32[8,18,1,512]{3,0,2,1:T(8,128)S(1)}, f32[8,18,1,512]{3,0,2,1:T(8,128)S(1)}, u32[]{:S(2)}, u32[]{:S(2)}) collective-permute-start(f32[8,18,1,512]{3,0,2,1:T(8,128)S(1)} %get-tuple-element.34), channel_id=1, source_target_pairs={{1,0},{2,1},{3,2},{4,3},{5,4},{6,5},{7,6},{8,7},{9,8},{10,9},{11,1... | collective-permute-start | bytes 884744 | tf_op jit(solution)/shard_map/ppermute | solution.py:28
  132.1 4.0 %collective-permute-start.15 = (f32[8,18,1,512]{3,0,2,1:T(8,128)S(1)}, f32[8,18,1,512]{3,0,2,1:T(8,128)S(1)}, u32[]{:S(2)}, u32[]{:S(2)}) collective-permute-start(f32[8,18,1,512]{3,0,2,1:T(8,128)S(1)} %get-tuple-element.35), channel_id=1, source_target_pairs={{0,1},{1,2},{2,3},{3,4},{4,5},{5,6},{6,7},{7,8},{8,9},{9,10},{10,1... | collective-permute-start | bytes 884744 | tf_op jit(solution)/shard_map/ppermute | solution.py:25
where the time goes:
time: 196 us
  other arithmetic  43 us (22%)
  starting transfers between devices  42.8 us (22%)
  local copies, waits for them, and re-layouts  42.4 us (22%)
  blocking collectives  39 us (20%)
  waiting for transfers between devices  26.3 us (13%)
  between operations  2.17 us (1%)
    psum x5, blocking collectives, over_axes(): return functools.reduce(lax.psum, axes, array)  39 us
    ppermute x8, starting transfers between devices, extended(): lax.ppermute(lax.slice_in_dim(block, 0, width, axis=dim), axis, backward)  33.1 us
    slice x8, local copies, waits for them, and re-layouts, scaled_apply(): beside = beside + jnp.roll(core, 1, 3) + jnp.roll(core, -1, 3)  22.9 us
    sub x2, other arithmetic, local(): t_next = 2.0 * scaled_apply(with_rim(t_high), energy, center, width) - t_low  21.1 us
    unnamed x36, local copies, waits for them, and re-layouts  18.3 us
    reduce_sum x2, other arithmetic, inner_pair(): square = jnp.sum(t_low * t_low, axis=(1, 2, 3))  13.6 us
    ppermute x8, waiting for transfers between devices, extended(): lax.ppermute(lax.slice_in_dim(block, 0, width, axis=dim), axis, backward)  13.3 us
    ppermute x8, waiting for transfers between devices, extended(): lax.ppermute(lax.slice_in_dim(block, block.shape[dim] - width, None, axis...  13 us
  transfers between devices with their start and end apart: 16, of which 11 were waited for; matrix products, arithmetic and copies ran while one was open for 14% of the time, Pallas kernels for 0%

commit v1 on v0

v1 whole, which is shorter than its diff:
```python
import functools

import jax
import jax.numpy as jnp
from jax import lax
from jax.experimental import pallas as pl
from jax.experimental.pallas import tpu as pltpu
from jax.sharding import PartitionSpec as P

STEPS = 4
MESH = pl.DeviceIdType.MESH


def kernel(
    counts, center_ref, width_ref, probes_ref, disorder_ref, last_ref, sums_ref,
    field, last, energy, rim_y, edge_y, parts, load_sem, store_sem, send_sem, recv_sem
):
    probes, rows_x, rows_y, rows_z = probes_ref.shape
    n_gx, n_gy = counts
    gx, gy = lax.axis_index("gx"), lax.axis_index("gy")
    beside = (
        (lax.rem(gx + 1, n_gx), gy),
        (lax.rem(gx + n_gx - 1, n_gx), gy),
        (gx, lax.rem(gy + 1, n_gy)),
        (gx, lax.rem(gy + n_gy - 1, n_gy)),
    )

    def load(p):
        return pltpu.make_async_copy(
            probes_ref.at[p], field.at[0, p, pl.ds(1, rows_x)], load_sem.at[p]
        )

    def store(p):
        return pltpu.make_async_copy(last.at[p], last_ref.at[p], store_sem.at[p])

    def load_energy():
        return pltpu.make_async_copy(disorder_ref, energy, load_sem.at[probes])

    for p in range(probes):
        load(p).start()
    load_energy().start()

    barrier = pltpu.get_barrier_semaphore()
    for x, y in beside:
        pl.semaphore_signal(barrier, inc=1, device_id={"gx": x, "gy": y}, device_id_type=MESH)

    def sends(n, p):
        faces = (
            (field.at[n, p, rows_x], field.at[n, p, 0]),
            (field.at[n, p, 1], field.at[n, p, rows_x + 1]),
            (edge_y.at[n, p, 1], rim_y.at[n, p, 0]),
            (edge_y.at[n, p, 0], rim_y.at[n, p, 1]),
        )
        return [
            pltpu.make_async_remote_copy(
                src_ref=src,
                dst_ref=dst,
                send_sem=send_sem.at[n, p, f],
                recv_sem=recv_sem.at[n, p, f],
                device_id={"gx": beside[f][0], "gy": beside[f][1]},
                device_id_type=MESH,
            )
            for f, (src, dst) in enumerate(faces)
        ]

    for p in range(probes):
        load(p).wait()

        def pack(x, carry):
            edge_y[0, p, 0, pl.ds(x, 1), :] = field[0, p, x + 1, 0:1, :]
            edge_y[0, p, 1, pl.ds(x, 1), :] = field[0, p, x + 1, rows_y - 1 : rows_y, :]
            return carry

        lax.fori_loop(0, rows_x, pack, 0)
    load_energy().wait()
    energy[...] = energy[...] - center_ref[0]
    pl.semaphore_wait(barrier, 4)

    def first(p, carry):
        for copy in sends(0, p):
            copy.start()
        return carry

    lax.fori_loop(0, probes, first, 0)

    row = lax.broadcasted_iota(jnp.int32, (rows_y, rows_z), 0)
    scale = 1.0 / width_ref[0]

    def fold(square):
        total = square[0:8]
        for start in range(8, rows_y, 8):
            total = total + square[start : start + 8]
        out = total[:, 0:128]
        for start in range(128, rows_z, 128):
            out = out + total[:, start : start + 128]
        return out

    for n in range(STEPS):

        def probe(p, carry):
            for copy in sends(n, p):
                copy.wait_recv()

            def plane(x, acc):
                square, cross = acc
                core = field[n, p, x + 1]
                total = field[n, p, x] + field[n, p, x + 2]
                low = jnp.where(row == 0, rim_y[n, p, 0, pl.ds(x, 1), :], pltpu.roll(core, 1, 0))
                high = jnp.where(
                    row == rows_y - 1, rim_y[n, p, 1, pl.ds(x, 1), :], pltpu.roll(core, rows_y - 1, 0)
                )
                total = total + (low + high)
                total = total + (pltpu.roll(core, 1, 1) + pltpu.roll(core, rows_z - 1, 1))
                new = (energy[x] * core - total) * (scale if n == 0 else 2.0 * scale)
                if n > 0:
                    new = new - field[n - 1, p, x + 1]
                if n + 1 < STEPS:
                    field[n + 1, p, x + 1] = new
                    edge_y[n + 1, p, 0, pl.ds(x, 1), :] = new[0:1]
                    edge_y[n + 1, p, 1, pl.ds(x, 1), :] = new[rows_y - 1 : rows_y]
                else:
                    last[p, x] = new
                return square + fold(core * core), cross + fold(new * core)

            zero = jnp.zeros((8, 128), jnp.float32)
            square, cross = lax.fori_loop(0, rows_x, plane, (zero, zero))
            parts[2 * n, p] = square
            parts[2 * n + 1, p] = cross
            if n + 1 < STEPS:
                for copy in sends(n + 1, p):
                    copy.start()
            else:
                store(p).start()
            return carry

        lax.fori_loop(0, probes, probe, 0)

    lane = lax.broadcasted_iota(jnp.int32, (probes, 128), 1)
    sums = jnp.zeros((probes, 128), jnp.float32)
    for j in range(2 * STEPS):
        column = jnp.sum(jnp.sum(parts[j], axis=1), axis=1, keepdims=True)
        sums = jnp.where(lane == j, column, sums)
    sums_ref[...] = sums

    def drain(p, carry):
        for n in range(STEPS):
            for copy in sends(n, p):
                copy.wait_send()
        store(p).wait()
        return carry

    lax.fori_loop(0, probes, drain, 0)


def solution(mesh):
    counts = (mesh.shape["gx"], mesh.shape["gy"])

    def local(probes, disorder, spectrum_center, half_width):
        n_probes, rows_x, rows_y, rows_z = probes.shape
        smem = pl.BlockSpec(memory_space=pltpu.SMEM)
        hbm = pl.BlockSpec(memory_space=pl.ANY)
        last, sums = pl.pallas_call(
            functools.partial(kernel, counts),
            out_shape=(
                jax.ShapeDtypeStruct(probes.shape, jnp.float32),
                jax.ShapeDtypeStruct((n_probes, 128), jnp.float32),
            ),
            in_specs=[smem, smem, hbm, hbm],
            out_specs=(hbm, pl.BlockSpec(memory_space=pltpu.VMEM)),
            scratch_shapes=[
                pltpu.VMEM((STEPS, n_probes, rows_x + 2, rows_y, rows_z), jnp.float32),
                pltpu.VMEM((n_probes, rows_x, rows_y, rows_z), jnp.float32),
                pltpu.VMEM((rows_x, rows_y, rows_z), jnp.float32),
                pltpu.VMEM((STEPS, n_probes, 2, rows_x, rows_z), jnp.float32),
                pltpu.VMEM((STEPS, n_probes, 2, rows_x, rows_z), jnp.float32),
                pltpu.VMEM((2 * STEPS, n_probes, 8, 128), jnp.float32),
                pltpu.SemaphoreType.DMA((n_probes + 1,)),
                pltpu.SemaphoreType.DMA((n_probes,)),
                pltpu.SemaphoreType.DMA((STEPS, n_probes, 4)),
                pltpu.SemaphoreType.DMA((STEPS, n_probes, 4)),
            ],
            compiler_params=pltpu.CompilerParams(
                collective_id=0, has_side_effects=True, vmem_limit_bytes=48 * 1024 * 1024
            ),
        )(spectrum_center, half_width, probes, disorder)
        sums = lax.psum(sums[:, : 2 * STEPS], ("gx", "gy"))
        sites = jnp.float32(
            rows_x * counts[0] * rows_y * counts[1] * rows_z
        )
        mean = sums / sites
        base = jnp.tile(mean[:, :2], (1, STEPS))
        return last, 2.0 * mean - base

    return jax.shard_map(
        local,
        mesh=mesh,
        in_specs=(P(None, "gx", "gy", None), P("gx", "gy", None), P(), P()),
        out_specs=(P(None, "gx", "gy", None), P()),
        check_vma=False,
    )
```

time: 196 us -> 157 us (0.80)
  Pallas kernels: 0 us -> 81.5 us
  starting transfers between devices: 42.8 us -> 0 us
  other arithmetic: 43 us -> 0.6 us
  local copies, waits for them, and re-layouts: 42.4 us -> 8.17 us
  waiting for transfers between devices: 26.3 us -> 0 us
  blocking collectives: 39 us -> 64.4 us
    pallas_call x0 -> x1, Pallas kernels: none -> 81.5 us  [local(): pl.pallas_call(functools.partial(kernel, counts), out_shape=(jax.ShapeDty...]
    ppermute x16 -> x0, starting transfers between devices: 42.8 us -> none  [the longest x8 33.1 us: extended(): lax.ppermute(lax.slice_in_dim(block, 0, width, axis=dim), axis, backward)]
    ppermute x16 -> x0, waiting for transfers between devices: 26.3 us -> none  [the longest x8 13.3 us: extended(): lax.ppermute(lax.slice_in_dim(block, 0, width, axis=dim), axis, backward)]
    psum x5 -> x1, blocking collectives: 39 us -> 64.4 us  [local(): sums = lax.psum(sums[:, :2 * STEPS], ('gx', 'gy'))]
    slice x14 -> x1, local copies, waits for them, and re-layouts: 24.1 us -> 0.08 us  [local(): base = jnp.tile(mean[:, :2], (1, STEPS))]
    sub x4 -> x1, other arithmetic: 21.1 us -> 0.6 us  [local(): return (last, 2.0 * mean - base)]
    reduce_sum x2 -> x0, other arithmetic: 13.6 us -> none  [inner_pair(): square = jnp.sum(t_low * t_low, axis=(1, 2, 3))]
    unnamed x36 -> x5, local copies, waits for them, and re-layouts: 18.3 us -> 8.01 us
  transfers between devices with their start and end apart: 16 -> 0, of which waited for: 11 -> 0; matrix products, arithmetic and copies ran while one was open for 14% -> 0% of each run, Pallas kernels for 0% -> 0%
where the time goes in v1:
time: 157 us
  Pallas kernels  81.5 us (52%)
  blocking collectives  64.4 us (41%)
  local copies, waits for them, and re-layouts  8.17 us (5%)
  between operations  1.95 us (1%)
    pallas_call x1, Pallas kernels, local(): pl.pallas_call(functools.partial(kernel, counts), out_shape=(jax.ShapeDty...  81.5 us
    psum x1, blocking collectives, local(): sums = lax.psum(sums[:, :2 * STEPS], ('gx', 'gy'))  64.4 us
    unnamed x5, local copies, waits for them, and re-layouts  8.01 us

profile of v1, /device:TPU:1, one launch (start us, length us, event | category | flops | bytes accessed | tf_op | source)
XLA Modules:
  0.0 156.6 jit_solution(2688887732288573234)
XLA Ops:
  1.9 0.0 copy-start.1
  1.9 1.0 copy-done.1
  3.0 81.5 %shard_map.59 = (f32[8,16,16,512]{3,2,1,0:T(8,128)S(1)}, f32[8,128]{1,0:T(8,128)S(1)}) custom-call(f32[1]{0:T(128)S(6)} %copy.9.center_ref, f32[1]{0:T(128)S(6)} %copy.10.width_ref, f32[8,16,16,512]{3,2,1,0:T(8,128)} %probes_ref.1, f32[16,16,512]{2,1,0:T(8,128)S(1)} %copy-done.1), custom_call_target="tpu_custom_call" | custom-call | tf_op jit(solution)/shard_map/pallas_call | solution.py:162
  84.5 0.0 copy-start
  84.5 1.9 %copy-done = f32[8,16,16,512]{3,2,1,0:T(8,128)} copy-done((f32[8,16,16,512]{3,2,1,0:T(8,128)}, f32[8,16,16,512]{3,2,1,0:T(8,128)S(1)}, u32[]{:S(2)}) %copy-start) | copy-done | bytes 4194328
  86.4 64.4 %psum.7 = f32[8,8]{1,0:T(8,128)S(1)} all-reduce(f32[8,8]{1,0:T(8,128)S(1)} %bitcast.3), channel_id=1, replica_groups=mesh['gx'=8,'gy'=16] {'gx','gy'}, use_global_device_ids=true, to_apply=%region_0.0 | all-reduce | flops 64 | bytes 512 | tf_op jit(solution)/shard_map/psum | solution.py:186
  150.8 0.1 copy.6
  150.9 0.1 copy.7
  151.0 0.6 multiply_subtract_fusion
  151.6 5.0 %copy.11 = f32[8,16,16,512]{3,2,1,0:T(8,128)} copy(f32[8,16,16,512]{3,2,1,0:T(8,128)} %copy-done) | data formatting | bytes 8388608
  (2 shorter events, 0.0 us)
Async XLA Ops:
  1.9 1.0 copy-start.1
  84.5 1.9 %copy-start = (f32[8,16,16,512]{3,2,1,0:T(8,128)}, f32[8,16,16,512]{3,2,1,0:T(8,128)S(1)}, u32[]{:S(2)}) copy-start(f32[8,16,16,512]{3,2,1,0:T(8,128)S(1)} %get-tuple-element.8) | copy-start | bytes 12582916

commit v2 on v1

--- a/solution.py
+++ b/solution.py
@@ -13,7 +13,8 @@
 
 def kernel(
     counts, center_ref, width_ref, probes_ref, disorder_ref, last_ref, sums_ref,
-    field, last, energy, rim_y, edge_y, parts, load_sem, store_sem, send_sem, recv_sem
+    field, energy, rim_y, edge_y, parts, slots, load_sem, send_sem, recv_sem,
+    slot_send, slot_recv
 ):
     probes, rows_x, rows_y, rows_z = probes_ref.shape
     n_gx, n_gy = counts
@@ -30,9 +31,6 @@
             probes_ref.at[p], field.at[0, p, pl.ds(1, rows_x)], load_sem.at[p]
         )
 
-    def store(p):
-        return pltpu.make_async_copy(last.at[p], last_ref.at[p], store_sem.at[p])
-
     def load_energy():
         return pltpu.make_async_copy(disorder_ref, energy, load_sem.at[probes])
 
@@ -40,8 +38,29 @@
         load(p).start()
     load_energy().start()
 
+    x_lo, x_hi, core = lax.rem(gx, 2), lax.rem(gy // 2, 2), lax.rem(gy, 2)
+    chip_x, chip_y, chip_z = 2 * x_hi + x_lo, gy // 4, gx // 2
+    wide_y, wide_z = n_gy // 4, n_gx // 2
+
+    def device(x, y, z, c):
+        return (2 * z + lax.rem(x, 2), 4 * y + 2 * (x // 2) + c)
+
+    groups = [[], [], []]
+    for step in range(1, 8):
+        x, c = lax.rem(chip_x + step // 2, 4), lax.rem(core + step, 2)
+        groups[0].append((device(x, chip_y, chip_z, c), 2 * x + c))
+    for step in range(1, wide_y):
+        y = lax.rem(chip_y + step, wide_y)
+        groups[1].append((device(chip_x, y, chip_z, core), y))
+    for step in range(1, wide_z):
+        z = lax.rem(chip_z + step, wide_z)
+        groups[2].append((device(chip_x, chip_y, z, core), z))
+    places = (2 * chip_x + core, chip_y, chip_z)
+    sizes = (8, wide_y, wide_z)
+
     barrier = pltpu.get_barrier_semaphore()
-    for x, y in beside:
+    greeted = list(beside) + [peer for group in groups for peer, _ in group]
+    for x, y in greeted:
         pl.semaphore_signal(barrier, inc=1, device_id={"gx": x, "gy": y}, device_id_type=MESH)
 
     def sends(n, p):
@@ -74,7 +93,7 @@
         lax.fori_loop(0, rows_x, pack, 0)
     load_energy().wait()
     energy[...] = energy[...] - center_ref[0]
-    pl.semaphore_wait(barrier, 4)
+    pl.semaphore_wait(barrier, len(greeted))
 
     def first(p, carry):
         for copy in sends(0, p):
@@ -119,7 +138,7 @@
                     edge_y[n + 1, p, 0, pl.ds(x, 1), :] = new[0:1]
                     edge_y[n + 1, p, 1, pl.ds(x, 1), :] = new[rows_y - 1 : rows_y]
                 else:
-                    last[p, x] = new
+                    last_ref[p, x] = new
                 return square + fold(core * core), cross + fold(new * core)
 
             zero = jnp.zeros((8, 128), jnp.float32)
@@ -129,8 +148,6 @@
             if n + 1 < STEPS:
                 for copy in sends(n + 1, p):
                     copy.start()
-            else:
-                store(p).start()
             return carry
 
         lax.fori_loop(0, probes, probe, 0)
@@ -140,16 +157,61 @@
     for j in range(2 * STEPS):
         column = jnp.sum(jnp.sum(parts[j], axis=1), axis=1, keepdims=True)
         sums = jnp.where(lane == j, column, sums)
+
+    for g, group in enumerate(groups):
+        place = places[g]
+        slots[g, place] = sums
+        copies = [
+            pltpu.make_async_remote_copy(
+                src_ref=slots.at[g, place],
+                dst_ref=slots.at[g, place],
+                send_sem=slot_send.at[g, i],
+                recv_sem=slot_recv.at[g, place],
+                device_id={"gx": peer[0], "gy": peer[1]},
+                device_id_type=MESH,
+            )
+            for i, (peer, _) in enumerate(group)
+        ]
+        for copy in copies:
+            copy.start()
+        for peer, slot in group:
+            pltpu.make_async_remote_copy(
+                src_ref=slots.at[g, slot],
+                dst_ref=slots.at[g, slot],
+                send_sem=slot_send.at[g, 0],
+                recv_sem=slot_recv.at[g, slot],
+                device_id={"gx": peer[0], "gy": peer[1]},
+                device_id_type=MESH,
+            ).wait_recv()
+        sums = slots[g, 0]
+        for i in range(1, sizes[g]):
+            sums = sums + slots[g, i]
+        for copy in copies:
+            copy.wait_send()
     sums_ref[...] = sums
 
     def drain(p, carry):
         for n in range(STEPS):
             for copy in sends(n, p):
                 copy.wait_send()
-        store(p).wait()
         return carry
 
     lax.fori_loop(0, probes, drain, 0)
+
+
+def finish(sites, last_ref, sums_ref, out_ref, moments_ref, sem):
+    probes = last_ref.shape[0]
+    copies = [
+        pltpu.make_async_copy(last_ref.at[p], out_ref.at[p], sem.at[p]) for p in range(probes)
+    ]
+    for copy in copies:
+        copy.start()
+    mean = sums_ref[...] * (1.0 / sites)
+    lane = lax.broadcasted_iota(jnp.int32, mean.shape, 1)
+    base = jnp.where(lax.rem(lane, 2) == 0, mean[:, 0:1], mean[:, 1:2])
+    moments_ref[...] = (2.0 * mean - base)[:, : 2 * STEPS]
+    for copy in copies:
+        copy.wait()
 
 
 def solution(mesh):
@@ -158,7 +220,8 @@
     def local(probes, disorder, spectrum_center, half_width):
         n_probes, rows_x, rows_y, rows_z = probes.shape
         smem = pl.BlockSpec(memory_space=pltpu.SMEM)
-        hbm = pl.BlockSpec(memory_space=pl.ANY)
+        vmem = pl.BlockSpec(memory_space=pltpu.VMEM)
+        hbm = pl.BlockSpec(memory_space=pltpu.HBM)
         last, sums = pl.pallas_call(
             functools.partial(kernel, counts),
             out_shape=(
@@ -166,30 +229,36 @@
                 jax.ShapeDtypeStruct((n_probes, 128), jnp.float32),
             ),
             in_specs=[smem, smem, hbm, hbm],
-            out_specs=(hbm, pl.BlockSpec(memory_space=pltpu.VMEM)),
+            out_specs=(vmem, vmem),
             scratch_shapes=[
                 pltpu.VMEM((STEPS, n_probes, rows_x + 2, rows_y, rows_z), jnp.float32),
-                pltpu.VMEM((n_probes, rows_x, rows_y, rows_z), jnp.float32),
                 pltpu.VMEM((rows_x, rows_y, rows_z), jnp.float32),
                 pltpu.VMEM((STEPS, n_probes, 2, rows_x, rows_z), jnp.float32),
                 pltpu.VMEM((STEPS, n_probes, 2, rows_x, rows_z), jnp.float32),
                 pltpu.VMEM((2 * STEPS, n_probes, 8, 128), jnp.float32),
+                pltpu.VMEM((3, 8, n_probes, 128), jnp.float32),
                 pltpu.SemaphoreType.DMA((n_probes + 1,)),
-                pltpu.SemaphoreType.DMA((n_probes,)),
                 pltpu.SemaphoreType.DMA((STEPS, n_probes, 4)),
                 pltpu.SemaphoreType.DMA((STEPS, n_probes, 4)),
+                pltpu.SemaphoreType.DMA((3, 8)),
+                pltpu.SemaphoreType.DMA((3, 8)),
             ],
             compiler_params=pltpu.CompilerParams(
                 collective_id=0, has_side_effects=True, vmem_limit_bytes=48 * 1024 * 1024
             ),
         )(spectrum_center, half_width, probes, disorder)
-        sums = lax.psum(sums[:, : 2 * STEPS], ("gx", "gy"))
-        sites = jnp.float32(
-            rows_x * counts[0] * rows_y * counts[1] * rows_z
-        )
-        mean = sums / sites
-        base = jnp.tile(mean[:, :2], (1, STEPS))
-        return last, 2.0 * mean - base
+        sites = rows_x * counts[0] * rows_y * counts[1] * rows_z
+        return pl.pallas_call(
+            functools.partial(finish, sites),
+            out_shape=(
+                jax.ShapeDtypeStruct(probes.shape, jnp.float32),
+                jax.ShapeDtypeStruct((n_probes, 2 * STEPS), jnp.float32),
+            ),
+            in_specs=[vmem, vmem],
+            out_specs=(hbm, vmem),
+            scratch_shapes=[pltpu.SemaphoreType.DMA((n_probes,))],
+            compiler_params=pltpu.CompilerParams(vmem_limit_bytes=8 * 1024 * 1024),
+        )(last, sums)
 
     return jax.shard_map(
         local,

time: 157 us -> 97.8 us (0.62)
  blocking collectives: 64.4 us -> 0 us
  Pallas kernels: 81.5 us -> 93.6 us
  local copies, waits for them, and re-layouts: 8.17 us -> 1.03 us
    psum x1 -> x0, blocking collectives: 64.4 us -> none  [local(): sums = lax.psum(sums[:, :2 * STEPS], ('gx', 'gy'))]
    pallas_call x1, Pallas kernels: 81.5 us -> 90.9 us  [local(): pl.pallas_call(functools.partial(kernel, counts), out_shape=(jax.ShapeDty...]
    unnamed x5 -> x2, local copies, waits for them, and re-layouts: 8.01 us -> 1.03 us
    pallas_call x0 -> x1, Pallas kernels: none -> 2.66 us  [local(): pl.pallas_call(functools.partial(finish, sites), out_shape=(jax.ShapeDtyp...]
where the time goes in v2:
time: 97.8 us; the launch traced here: 96.6 us
  Pallas kernels  93.6 us (96%)
  between operations  1.94 us (2%)
  local copies, waits for them, and re-layouts  1.03 us (1%)
    pallas_call x1, Pallas kernels, local(): pl.pallas_call(functools.partial(kernel, counts), out_shape=(jax.ShapeDty...  90.9 us
    pallas_call x1, Pallas kernels, local(): pl.pallas_call(functools.partial(finish, sites), out_shape=(jax.ShapeDtyp...  2.66 us

profile of v2, /device:TPU:1, one launch (start us, length us, event | category | flops | bytes accessed | tf_op | source)
XLA Modules:
  0.0 96.6 jit_solution(4269000204256569232)
XLA Ops:
  1.9 0.0 copy-start
  1.9 1.0 %copy-done = f32[16,16,512]{2,1,0:T(8,128)S(1)} copy-done((f32[16,16,512]{2,1,0:T(8,128)S(1)}, f32[16,16,512]{2,1,0:T(8,128)}, u32[]{:S(2)}) %copy-start) | copy-done | bytes 524312
  3.0 90.9 %shard_map.59 = (f32[8,16,16,512]{3,2,1,0:T(8,128)S(1)}, f32[8,128]{1,0:T(8,128)S(1)}) custom-call(f32[1]{0:T(128)S(6)} %copy.6.center_ref, f32[1]{0:T(128)S(6)} %copy.7.width_ref, f32[8,16,16,512]{3,2,1,0:T(8,128)} %probes_ref.1, f32[16,16,512]{2,1,0:T(8,128)S(1)} %copy-done), custom_call_target="tpu_custom_call" | custom-call | tf_op jit(solution)/shard_map/pallas_call | solution.py:225
  93.9 2.7 %shard_map.60 = (f32[8,16,16,512]{3,2,1,0:T(8,128)}, f32[8,8]{1,0:T(8,128)}) custom-call(f32[8,16,16,512]{3,2,1,0:T(8,128)S(1)} %get-tuple-element.4.last_ref, f32[8,128]{1,0:T(8,128)S(1)} %get-tuple-element.5.sums_ref), custom_call_target="tpu_custom_call" | custom-call | tf_op jit(solution)/shard_map/pallas_call | solution.py:251
Async XLA Ops:
  1.9 1.0 %copy-start = (f32[16,16,512]{2,1,0:T(8,128)S(1)}, f32[16,16,512]{2,1,0:T(8,128)}, u32[]{:S(2)}) copy-start(f32[16,16,512]{2,1,0:T(8,128)} %disorder_ref.1) | copy-start | bytes 1572868

commit v3 on v2

v3 whole, which is shorter than its diff:
```python
import functools

import jax
import jax.numpy as jnp
from jax import lax
from jax.experimental import pallas as pl
from jax.experimental.pallas import tpu as pltpu
from jax.sharding import PartitionSpec as P

STEPS = 4
BATCH = 1
MESH = pl.DeviceIdType.MESH
LEAD = 4
UNROLL = 8
LATER = (2, 2, 8)
FINISH = (2, 2, 8)
VMEM_LIMIT = 48 * 1024 * 1024


def kernel(
    counts, center_ref, width_ref, probes_ref, disorder_ref, last_ref, sums_ref,
    field, energy, rim_y, edge_y, parts, slots, load_sem, send_sem, recv_sem,
    slot_send, slot_recv
):
    probes, rows_x, rows_y, rows_z = probes_ref.shape
    batches = probes // BATCH
    n_gx, n_gy = counts
    gx, gy = lax.axis_index("gx"), lax.axis_index("gy")
    beside = (
        (lax.rem(gx + 1, n_gx), gy),
        (lax.rem(gx + n_gx - 1, n_gx), gy),
        (gx, lax.rem(gy + 1, n_gy)),
        (gx, lax.rem(gy + n_gy - 1, n_gy)),
    )
    x_lo, x_hi, core = lax.rem(gx, 2), lax.rem(gy // 2, 2), lax.rem(gy, 2)
    chip_x, chip_y, chip_z = 2 * x_hi + x_lo, gy // 4, gx // 2
    wide_y, wide_z = n_gy // 4, n_gx // 2

    def device(x, y, z, c):
        return (2 * z + lax.rem(x, 2), 4 * y + 2 * (x // 2) + c)

    group_x, group_y, group_z = [], [], []
    for step in range(1, 8):
        x, c = lax.rem(chip_x + step // 2, 4), lax.rem(core + step, 2)
        group_x.append(device(x, chip_y, chip_z, c))
    for step in range(1, wide_y):
        group_y.append(device(chip_x, lax.rem(chip_y + step, wide_y), chip_z, core))
    for step in range(1, wide_z):
        group_z.append(device(chip_x, chip_y, lax.rem(chip_z + step, wide_z), core))
    groups = ((group_z, chip_z), (group_y, chip_y), (group_x, 2 * chip_x + core))

    barrier = pltpu.get_barrier_semaphore()
    greeted = list(beside) + group_z + group_y + group_x
    for x, y in greeted:
        pl.semaphore_signal(barrier, inc=1, device_id={"gx": x, "gy": y}, device_id_type=MESH)

    def load(p):
        return pltpu.make_async_copy(
            probes_ref.at[p], field.at[0, p, pl.ds(1, rows_x)], load_sem.at[p]
        )

    def load_energy():
        return pltpu.make_async_copy(disorder_ref, energy, load_sem.at[probes])

    for p in range(probes):
        load(p).start()
    load_energy().start()

    def faces(n, b):
        group = pl.ds(b * BATCH, BATCH)
        return (
            (field.at[n, group, rows_x], field.at[n, group, 0]),
            (field.at[n, group, 1], field.at[n, group, rows_x + 1]),
            (edge_y.at[n, 1, group], rim_y.at[n, 0, group]),
            (edge_y.at[n, 0, group], rim_y.at[n, 1, group]),
        )

    def send(n, b, which, sem):
        for f in which:
            src, dst = faces(n, b)[f]
            pltpu.make_async_remote_copy(
                src_ref=src,
                dst_ref=dst,
                send_sem=send_sem.at[sem, b],
                recv_sem=recv_sem.at[sem, b],
                device_id={"gx": beside[f][0], "gy": beside[f][1]},
                device_id_type=MESH,
            ).start()

    def settled(b, count, sem):
        whole = field.at[0, 0, pl.ds(0, count * BATCH)]
        return pltpu.make_async_remote_copy(
            src_ref=whole,
            dst_ref=whole,
            send_sem=send_sem.at[sem, b],
            recv_sem=recv_sem.at[sem, b],
            device_id={"gx": beside[0][0], "gy": beside[0][1]},
            device_id_type=MESH,
        )

    for p in range(probes):
        load(p).wait()

        def pack(x, carry):
            edge_y[0, 0, p, pl.ds(x, 1), :] = field[0, p, x + 1, 0:1, :]
            edge_y[0, 1, p, pl.ds(x, 1), :] = field[0, p, x + 1, rows_y - 1 : rows_y, :]
            return carry

        lax.fori_loop(0, rows_x, pack, 0)
    load_energy().wait()
    energy[...] = energy[...] - center_ref[0]
    pl.semaphore_wait(barrier, len(greeted))

    for b in range(batches):
        send(0, b, (0, 1, 2, 3), 0)

    row = lax.broadcasted_iota(jnp.int32, (rows_y, rows_z), 0)
    scale = 1.0 / width_ref[0]
    zero = jnp.zeros((8, 128), jnp.float32)

    def fold(product):
        total = product[0:8]
        for start in range(8, rows_y, 8):
            total = total + product[start : start + 8]
        out = total[:, 0:128]
        for start in range(128, rows_z, 128):
            out = out + total[:, start : start + 128]
        return out

    def low_side(n, p, x, middle):
        y = jnp.where(row == 0, rim_y[n, 0, p, pl.ds(x, 1), :], pltpu.roll(middle, 1, 0))
        return field[n, p, x] + y + pltpu.roll(middle, 1, 1)

    def high_side(n, p, x, middle):
        y = jnp.where(
            row == rows_y - 1, rim_y[n, 1, p, pl.ds(x, 1), :], pltpu.roll(middle, rows_y - 1, 0)
        )
        return field[n, p, x + 2] + y + pltpu.roll(middle, rows_z - 1, 1)

    def advance(n, p):
        def plane(x, acc):
            square, cross = acc
            middle = field[n, p, x + 1]
            total = low_side(n, p, x, middle) + high_side(n, p, x, middle)
            new = (energy[x] * middle - total) * (scale if n == 0 else 2.0 * scale)
            if n > 0:
                new = new - field[n - 1, p, x + 1]
            field[n + 1, p, x + 1] = new
            edge_y[n + 1, 0, p, pl.ds(x, 1), :] = new[0:1]
            edge_y[n + 1, 1, p, pl.ds(x, 1), :] = new[rows_y - 1 : rows_y]
            return square + fold(middle * middle), cross + fold(new * middle)

        parts[2 * n, p], parts[2 * n + 1, p] = lax.fori_loop(0, rows_x, plane, (zero, zero), unroll=UNROLL)

    final = STEPS - 1

    def last_low(p):
        def plane(x, acc):
            square, cross = acc
            middle = field[final, p, x + 1]
            low = (2.0 * scale) * low_side(final, p, x, middle)
            new = (2.0 * scale) * energy[x] * middle - low - field[final - 1, p, x + 1]
            last_ref[p, x] = new
            return square + fold(middle * middle), cross + fold((new - low) * middle)

        parts[2 * final, p], parts[2 * final + 1, p] = lax.fori_loop(0, rows_x, plane, (zero, zero), unroll=UNROLL)

    def last_high(p):
        def plane(x, carry):
            middle = field[final, p, x + 1]
            last_ref[p, x] = last_ref[p, x] - (2.0 * scale) * high_side(final, p, x, middle)
            return carry

        lax.fori_loop(0, rows_x, plane, 0, unroll=UNROLL)

    for n in range(final):

        def batch(b, carry):
            settled(b, 4, n % 2).wait_recv()

            def one(q, carry):
                advance(n, b * BATCH + q)
                return carry

            lax.fori_loop(0, BATCH, one, 0)
            if n > 0:
                settled(b, 4, (n + 1) % 2).wait_send()
            send(n + 1, b, (0, 1, 2, 3) if n + 1 < final else (0, 2), (n + 1) % 2)
            return carry

        lax.fori_loop(0, batches, batch, 0)

    sent, done = [0], [0]

    def send_more(count):
        for _ in range(count):
            if sent[0] < batches:
                send(final, sent[0], (1, 3), 2)
                sent[0] += 1

    def finish_more(count):
        for _ in range(count):
            if done[0] < sent[0]:
                settled(done[0], 2, 2).wait_recv()

                def one(q, carry, b=done[0]):
                    last_high(b * BATCH + q)
                    return carry

                lax.fori_loop(0, BATCH, one, 0)
                done[0] += 1

    for b in range(batches):
        settled(b, 2, final % 2).wait_recv()

        def one(q, carry, b=b):
            last_low(b * BATCH + q)
            return carry

        lax.fori_loop(0, BATCH, one, 0)
        if b >= LEAD:
            send_more(1)

    lane = lax.broadcasted_iota(jnp.int32, (probes, 128), 1)
    sums = jnp.zeros((probes, 128), jnp.float32)
    for j in range(2 * STEPS):
        column = jnp.sum(jnp.sum(parts[j], axis=1), axis=1, keepdims=True)
        sums = jnp.where(lane == j, column, sums)

    for g, (group, place) in enumerate(groups):
        slots[g, place] = sums
        for x, y in group:
            pltpu.make_async_remote_copy(
                src_ref=slots.at[g, place],
                dst_ref=slots.at[g, place],
                send_sem=slot_send.at[g],
                recv_sem=slot_recv.at[g],
                device_id={"gx": x, "gy": y},
                device_id_type=MESH,
            ).start()
        send_more(LATER[g])
        finish_more(FINISH[g])
        whole = slots.at[g, pl.ds(0, len(group))]
        arrived = pltpu.make_async_remote_copy(
            src_ref=whole,
            dst_ref=whole,
            send_sem=slot_send.at[g],
            recv_sem=slot_recv.at[g],
            device_id={"gx": group[0][0], "gy": group[0][1]},
            device_id_type=MESH,
        )
        arrived.wait_recv()
        sums = slots[g, 0]
        for i in range(1, len(group) + 1):
            sums = sums + slots[g, i]
        arrived.wait_send()
    sums_ref[...] = sums
    finish_more(batches)

    for b in range(batches):
        settled(b, 4, (final - 1) % 2).wait_send()
        settled(b, 2, final % 2).wait_send()
        settled(b, 2, 2).wait_send()


def finish(sites, last_ref, sums_ref, out_ref, moments_ref, sem):
    probes = last_ref.shape[0]
    copies = [
        pltpu.make_async_copy(last_ref.at[p], out_ref.at[p], sem.at[p]) for p in range(probes)
    ]
    for copy in copies:
        copy.start()
    mean = sums_ref[...] * (1.0 / sites)
    lane = lax.broadcasted_iota(jnp.int32, mean.shape, 1)
    base = jnp.where(lax.rem(lane, 2) == 0, mean[:, 0:1], mean[:, 1:2])
    moments_ref[...] = (2.0 * mean - base)[:, : 2 * STEPS]
    for copy in copies:
        copy.wait()


def solution(mesh):
    counts = (mesh.shape["gx"], mesh.shape["gy"])

    def local(probes, disorder, spectrum_center, half_width):
        n_probes, rows_x, rows_y, rows_z = probes.shape
        disorder = pltpu.with_memory_space_constraint(disorder, pltpu.HBM)
        smem = pl.BlockSpec(memory_space=pltpu.SMEM)
        vmem = pl.BlockSpec(memory_space=pltpu.VMEM)
        hbm = pl.BlockSpec(memory_space=pltpu.HBM)
        last, sums = pl.pallas_call(
            functools.partial(kernel, counts),
            out_shape=(
                jax.ShapeDtypeStruct(probes.shape, jnp.float32),
                jax.ShapeDtypeStruct((n_probes, 128), jnp.float32),
            ),
            in_specs=[smem, smem, hbm, hbm],
            out_specs=(vmem, vmem),
            scratch_shapes=[
                pltpu.VMEM((STEPS, n_probes, rows_x + 2, rows_y, rows_z), jnp.float32),
                pltpu.VMEM((rows_x, rows_y, rows_z), jnp.float32),
                pltpu.VMEM((STEPS, 2, n_probes, rows_x, rows_z), jnp.float32),
                pltpu.VMEM((STEPS, 2, n_probes, rows_x, rows_z), jnp.float32),
                pltpu.VMEM((2 * STEPS, n_probes, 8, 128), jnp.float32),
                pltpu.VMEM((3, 8, n_probes, 128), jnp.float32),
                pltpu.SemaphoreType.DMA((n_probes + 1,)),
                pltpu.SemaphoreType.DMA((3, n_probes // BATCH)),
                pltpu.SemaphoreType.DMA((3, n_probes // BATCH)),
                pltpu.SemaphoreType.DMA((3,)),
                pltpu.SemaphoreType.DMA((3,)),
            ],
            compiler_params=pltpu.CompilerParams(
                collective_id=0, has_side_effects=True, vmem_limit_bytes=VMEM_LIMIT
            ),
        )(spectrum_center, half_width, probes, disorder)
        sites = rows_x * counts[0] * rows_y * counts[1] * rows_z
        return pl.pallas_call(
            functools.partial(finish, sites),
            out_shape=(
                jax.ShapeDtypeStruct(probes.shape, jnp.float32),
                jax.ShapeDtypeStruct((n_probes, 2 * STEPS), jnp.float32),
            ),
            in_specs=[vmem, vmem],
            out_specs=(hbm, vmem),
            scratch_shapes=[pltpu.SemaphoreType.DMA((n_probes,))],
            compiler_params=pltpu.CompilerParams(vmem_limit_bytes=8 * 1024 * 1024),
        )(last, sums)

    return jax.shard_map(
        local,
        mesh=mesh,
        in_specs=(P(None, "gx", "gy", None), P("gx", "gy", None), P(), P()),
        out_specs=(P(None, "gx", "gy", None), P()),
        check_vma=False,
    )
```

time: 97.8 us -> 85.8 us (0.88); the launches traced: 96.6 us -> 85.7 us
  Pallas kernels: 93.6 us -> 83.7 us
  local copies, waits for them, and re-layouts: 1.03 us -> 0 us
    pallas_call x1, Pallas kernels: 90.9 us -> 81.1 us  [local(): pl.pallas_call(functools.partial(kernel, counts), out_shape=(jax.ShapeDty...]
    unnamed x2 -> x0, local copies, waits for them, and re-layouts: 1.03 us -> none
where the time goes in v3:
time: 85.8 us; the launch traced here: 85.7 us
  Pallas kernels  83.7 us (98%)
  between operations  1.93 us (2%)
    pallas_call x1, Pallas kernels, local(): pl.pallas_call(functools.partial(kernel, counts), out_shape=(jax.ShapeDty...  81.1 us
    pallas_call x1, Pallas kernels, local(): pl.pallas_call(functools.partial(finish, sites), out_shape=(jax.ShapeDtyp...  2.66 us

profile of v3, /device:TPU:1, one launch (start us, length us, event | category | flops | bytes accessed | tf_op | source)
XLA Modules:
  0.0 85.7 jit_solution(18331924492044873073)
XLA Ops:
  1.9 81.1 %shard_map.59 = (f32[8,16,16,512]{3,2,1,0:T(8,128)S(1)}, f32[8,128]{1,0:T(8,128)S(1)}) custom-call(f32[1]{0:T(128)S(6)} %copy.6.center_ref, f32[1]{0:T(128)S(6)} %copy.7.width_ref, f32[8,16,16,512]{3,2,1,0:T(8,128)} %probes_ref.1, f32[16,16,512]{2,1,0:T(8,128)} %disorder_ref.1), custom_call_target="tpu_custom_call" | custom-call | tf_op jit(solution)/shard_map/pallas_call | solution.py:290
  83.0 2.7 %shard_map.60 = (f32[8,16,16,512]{3,2,1,0:T(8,128)}, f32[8,8]{1,0:T(8,128)}) custom-call(f32[8,16,16,512]{3,2,1,0:T(8,128)S(1)} %get-tuple-element.4.last_ref, f32[8,128]{1,0:T(8,128)S(1)} %get-tuple-element.5.sums_ref), custom_call_target="tpu_custom_call" | custom-call | tf_op jit(solution)/shard_map/pallas_call | solution.py:316

commit v4 on v3

--- a/solution.py
+++ b/solution.py
@@ -11,6 +11,7 @@
 BATCH = 1
 MESH = pl.DeviceIdType.MESH
 LEAD = 4
+ORDER = (0, 1, 2, 3)
 UNROLL = 8
 LATER = (2, 2, 8)
 FINISH = (2, 2, 8)
@@ -20,7 +21,7 @@
 def kernel(
     counts, center_ref, width_ref, probes_ref, disorder_ref, last_ref, sums_ref,
     field, energy, rim_y, edge_y, parts, slots, load_sem, send_sem, recv_sem,
-    slot_send, slot_recv
+    slot_send, slot_recv, ready
 ):
     probes, rows_x, rows_y, rows_z = probes_ref.shape
     batches = probes // BATCH
@@ -39,20 +40,31 @@
     def device(x, y, z, c):
         return (2 * z + lax.rem(x, 2), 4 * y + 2 * (x // 2) + c)
 
-    group_x, group_y, group_z = [], [], []
-    for step in range(1, 8):
-        x, c = lax.rem(chip_x + step // 2, 4), lax.rem(core + step, 2)
-        group_x.append(device(x, chip_y, chip_z, c))
-    for step in range(1, wide_y):
-        group_y.append(device(chip_x, lax.rem(chip_y + step, wide_y), chip_z, core))
-    for step in range(1, wide_z):
-        group_z.append(device(chip_x, chip_y, lax.rem(chip_z + step, wide_z), core))
+    def group(pairs):
+        return [device(lax.rem(chip_x + x, 4), lax.rem(chip_y + y, wide_y), lax.rem(chip_z + z, wide_z),
+                       lax.rem(core + c, 2)) for x, y, z, c in pairs]
+
+    group_x = group([(x, 0, 0, c) for x in range(4) for c in range(2) if x or c])
+    group_y = group([(0, y, 0, 0) for y in range(1, wide_y)])
+    group_z = group([(0, 0, z, 0) for z in range(1, wide_z)])
     groups = ((group_z, chip_z), (group_y, chip_y), (group_x, 2 * chip_x + core))
 
+    partner = (gx + 1 - 2 * x_lo, gy)
+    across = (lax.rem(gx + 2 * x_lo + n_gx - 1, n_gx), gy)
+    pairs = list(beside[2:]) + group_z + group_y + group([(2, 0, 0, 0), (0, 0, 0, 1), (2, 0, 0, 1)])
     barrier = pltpu.get_barrier_semaphore()
-    greeted = list(beside) + group_z + group_y + group_x
-    for x, y in greeted:
-        pl.semaphore_signal(barrier, inc=1, device_id={"gx": x, "gy": y}, device_id_type=MESH)
+
+    def tell(semaphore, peer):
+        pl.semaphore_signal(
+            semaphore, inc=1, device_id={"gx": peer[0], "gy": peer[1]}, device_id_type=MESH
+        )
+
+    @pl.when(x_lo == 1)
+    def _():
+        tell(barrier, partner)
+
+    for x, y in pairs:
+        tell(barrier, (x + 1 - lax.rem(x, 2), y))
 
     def load(p):
         return pltpu.make_async_copy(
@@ -75,17 +87,20 @@
             (edge_y.at[n, 0, group], rim_y.at[n, 1, group]),
         )
 
+    def start(src, dst, peer, sem, b):
+        pltpu.make_async_remote_copy(
+            src_ref=src,
+            dst_ref=dst,
+            send_sem=send_sem.at[sem, b],
+            recv_sem=recv_sem.at[sem, b],
+            device_id={"gx": peer[0], "gy": peer[1]},
+            device_id_type=MESH,
+        ).start()
+
     def send(n, b, which, sem):
         for f in which:
             src, dst = faces(n, b)[f]
-            pltpu.make_async_remote_copy(
-                src_ref=src,
-                dst_ref=dst,
-                send_sem=send_sem.at[sem, b],
-                recv_sem=recv_sem.at[sem, b],
-                device_id={"gx": beside[f][0], "gy": beside[f][1]},
-                device_id_type=MESH,
-            ).start()
+            start(src, dst, beside[f], sem, b)
 
     def settled(b, count, sem):
         whole = field.at[0, 0, pl.ds(0, count * BATCH)]
@@ -98,21 +113,52 @@
             device_id_type=MESH,
         )
 
-    for p in range(probes):
-        load(p).wait()
-
-        def pack(x, carry):
-            edge_y[0, 0, p, pl.ds(x, 1), :] = field[0, p, x + 1, 0:1, :]
-            edge_y[0, 1, p, pl.ds(x, 1), :] = field[0, p, x + 1, rows_y - 1 : rows_y, :]
-            return carry
-
-        lax.fori_loop(0, rows_x, pack, 0)
+    @pl.when(x_lo == 0)
+    def _():
+        pl.semaphore_wait(barrier, 1)
+        tell(ready.at[0], partner)
+
+    @pl.when(x_lo == 1)
+    def _():
+        pl.semaphore_wait(ready.at[0], 1)
+
+    for b in range(batches):
+        for p in range(b * BATCH, b * BATCH + BATCH):
+            load(p).wait()
+        which = pl.ds(b * BATCH, BATCH)
+        start(
+            field.at[0, which, rows_x - (rows_x - 1) * x_lo],
+            field.at[0, which, (rows_x + 1) * x_lo],
+            partner, 0, b,
+        )
+
+    def pack(p, carry):
+        for x in range(rows_x):
+            edge_y[0, 0, p, x : x + 1, :] = field[0, p, x + 1, 0:1, :]
+            edge_y[0, 1, p, x : x + 1, :] = field[0, p, x + 1, rows_y - 1 : rows_y, :]
+        return carry
+
+    lax.fori_loop(0, probes, pack, 0)
+
+    @pl.when(x_lo == 1)
+    def _():
+        pl.semaphore_wait(barrier, 2 * len(pairs))
+        tell(ready.at[1], partner)
+
+    @pl.when(x_lo == 0)
+    def _():
+        pl.semaphore_wait(ready.at[1], 1)
+
+    for b in range(batches):
+        which = pl.ds(b * BATCH, BATCH)
+        start(
+            field.at[0, which, 1 + (rows_x - 1) * x_lo],
+            field.at[0, which, (rows_x + 1) * (1 - x_lo)],
+            across, 0, b,
+        )
+        send(0, b, (2, 3), 0)
     load_energy().wait()
     energy[...] = energy[...] - center_ref[0]
-    pl.semaphore_wait(barrier, len(greeted))
-
-    for b in range(batches):
-        send(0, b, (0, 1, 2, 3), 0)
 
     row = lax.broadcasted_iota(jnp.int32, (rows_y, rows_z), 0)
     scale = 1.0 / width_ref[0]
@@ -185,7 +231,7 @@
             lax.fori_loop(0, BATCH, one, 0)
             if n > 0:
                 settled(b, 4, (n + 1) % 2).wait_send()
-            send(n + 1, b, (0, 1, 2, 3) if n + 1 < final else (0, 2), (n + 1) % 2)
+            send(n + 1, b, ORDER if n + 1 < final else (0, 2), (n + 1) % 2)
             return carry
 
         lax.fori_loop(0, batches, batch, 0)
@@ -210,6 +256,16 @@
                 lax.fori_loop(0, BATCH, one, 0)
                 done[0] += 1
 
+    lane = lax.broadcasted_iota(jnp.int32, (probes, 128), 1)
+
+    def column_sums(sums, columns):
+        for j in columns:
+            column = jnp.sum(jnp.sum(parts[j], axis=1), axis=1, keepdims=True)
+            sums = jnp.where(lane == j, column, sums)
+        return sums
+
+    sums = column_sums(jnp.zeros((probes, 128), jnp.float32), range(2 * final))
+
     for b in range(batches):
         settled(b, 2, final % 2).wait_recv()
 
@@ -221,15 +277,11 @@
         if b >= LEAD:
             send_more(1)
 
-    lane = lax.broadcasted_iota(jnp.int32, (probes, 128), 1)
-    sums = jnp.zeros((probes, 128), jnp.float32)
-    for j in range(2 * STEPS):
-        column = jnp.sum(jnp.sum(parts[j], axis=1), axis=1, keepdims=True)
-        sums = jnp.where(lane == j, column, sums)
-
-    for g, (group, place) in enumerate(groups):
+    sums = column_sums(sums, range(2 * final, 2 * STEPS))
+
+    for g, (peers, place) in enumerate(groups):
         slots[g, place] = sums
-        for x, y in group:
+        for x, y in peers:
             pltpu.make_async_remote_copy(
                 src_ref=slots.at[g, place],
                 dst_ref=slots.at[g, place],
@@ -240,18 +292,18 @@
             ).start()
         send_more(LATER[g])
         finish_more(FINISH[g])
-        whole = slots.at[g, pl.ds(0, len(group))]
+        whole = slots.at[g, pl.ds(0, len(peers))]
         arrived = pltpu.make_async_remote_copy(
             src_ref=whole,
             dst_ref=whole,
             send_sem=slot_send.at[g],
             recv_sem=slot_recv.at[g],
-            device_id={"gx": group[0][0], "gy": group[0][1]},
+            device_id={"gx": peers[0][0], "gy": peers[0][1]},
             device_id_type=MESH,
         )
         arrived.wait_recv()
         sums = slots[g, 0]
-        for i in range(1, len(group) + 1):
+        for i in range(1, len(peers) + 1):
             sums = sums + slots[g, i]
         arrived.wait_send()
     sums_ref[...] = sums
@@ -307,6 +359,7 @@
                 pltpu.SemaphoreType.DMA((3, n_probes // BATCH)),
                 pltpu.SemaphoreType.DMA((3,)),
                 pltpu.SemaphoreType.DMA((3,)),
+                pltpu.SemaphoreType.REGULAR((2,)),
             ],
             compiler_params=pltpu.CompilerParams(
                 collective_id=0, has_side_effects=True, vmem_limit_bytes=VMEM_LIMIT

time: 85.8 us -> 84.3 us (0.983)
  Pallas kernels: 83.7 us -> 82.3 us
    pallas_call x1, Pallas kernels: 81.1 us -> 79.6 us  [local(): pl.pallas_call(functools.partial(kernel, counts), out_shape=(jax.ShapeDty...]
where the time goes in v4:
time: 84.3 us; the launch traced here: 84.2 us
  Pallas kernels  82.3 us (98%)
  between operations  1.93 us (2%)
    pallas_call x1, Pallas kernels, local(): pl.pallas_call(functools.partial(kernel, counts), out_shape=(jax.ShapeDty...  79.6 us
    pallas_call x1, Pallas kernels, local(): pl.pallas_call(functools.partial(finish, sites), out_shape=(jax.ShapeDtyp...  2.66 us

profile of v4, /device:TPU:1, one launch (start us, length us, event | category | flops | bytes accessed | tf_op | source)
XLA Modules:
  0.0 84.2 jit_solution(943801226043576083)
XLA Ops:
  1.9 79.6 %shard_map.59 = (f32[8,16,16,512]{3,2,1,0:T(8,128)S(1)}, f32[8,128]{1,0:T(8,128)S(1)}) custom-call(f32[1]{0:T(128)S(6)} %copy.6.center_ref, f32[1]{0:T(128)S(6)} %copy.7.width_ref, f32[8,16,16,512]{3,2,1,0:T(8,128)} %probes_ref.1, f32[16,16,512]{2,1,0:T(8,128)} %disorder_ref.1), custom_call_target="tpu_custom_call" | custom-call | tf_op jit(solution)/shard_map/pallas_call | solution.py:342
  81.5 2.7 %shard_map.60 = (f32[8,16,16,512]{3,2,1,0:T(8,128)}, f32[8,8]{1,0:T(8,128)}) custom-call(f32[8,16,16,512]{3,2,1,0:T(8,128)S(1)} %get-tuple-element.4.last_ref, f32[8,128]{1,0:T(8,128)S(1)} %get-tuple-element.5.sums_ref), custom_call_target="tpu_custom_call" | custom-call | tf_op jit(solution)/shard_map/pallas_call | solution.py:369

commit v5 on v4

--- a/solution.py
+++ b/solution.py
@@ -10,11 +10,11 @@
 STEPS = 4
 BATCH = 1
 MESH = pl.DeviceIdType.MESH
-LEAD = 4
+LEAD = (5, 2)
 ORDER = (0, 1, 2, 3)
 UNROLL = 8
-LATER = (2, 2, 8)
-FINISH = (2, 2, 8)
+LATER = ((8, 8), (8, 8))
+FINISH = (4, 8)
 VMEM_LIMIT = 48 * 1024 * 1024
 
 
@@ -45,13 +45,12 @@
                        lax.rem(core + c, 2)) for x, y, z, c in pairs]
 
     group_x = group([(x, 0, 0, c) for x in range(4) for c in range(2) if x or c])
-    group_y = group([(0, y, 0, 0) for y in range(1, wide_y)])
-    group_z = group([(0, 0, z, 0) for z in range(1, wide_z)])
-    groups = ((group_z, chip_z), (group_y, chip_y), (group_x, 2 * chip_x + core))
+    group_yz = group([(0, y, z, 0) for y in range(wide_y) for z in range(wide_z) if y or z])
+    groups = ((group_yz, chip_y * wide_z + chip_z), (group_x, 2 * chip_x + core))
 
     partner = (gx + 1 - 2 * x_lo, gy)
     across = (lax.rem(gx + 2 * x_lo + n_gx - 1, n_gx), gy)
-    pairs = list(beside[2:]) + group_z + group_y + group([(2, 0, 0, 0), (0, 0, 0, 1), (2, 0, 0, 1)])
+    pairs = list(beside[2:]) + group_yz + group([(2, 0, 0, 0), (0, 0, 0, 1), (2, 0, 0, 1)])
     barrier = pltpu.get_barrier_semaphore()
 
     def tell(semaphore, peer):
@@ -74,8 +73,11 @@
     def load_energy():
         return pltpu.make_async_copy(disorder_ref, energy, load_sem.at[probes])
 
-    for p in range(probes):
+    def begin(p, carry):
         load(p).start()
+        return carry
+
+    lax.fori_loop(0, probes, begin, 0)
     load_energy().start()
 
     def faces(n, b):
@@ -122,15 +124,18 @@
     def _():
         pl.semaphore_wait(ready.at[0], 1)
 
-    for b in range(batches):
-        for p in range(b * BATCH, b * BATCH + BATCH):
-            load(p).wait()
+    def pair_first(b, carry):
+        for q in range(BATCH):
+            load(b * BATCH + q).wait()
         which = pl.ds(b * BATCH, BATCH)
         start(
             field.at[0, which, rows_x - (rows_x - 1) * x_lo],
             field.at[0, which, (rows_x + 1) * x_lo],
             partner, 0, b,
         )
+        return carry
+
+    lax.fori_loop(0, batches, pair_first, 0)
 
     def pack(p, carry):
         for x in range(rows_x):
@@ -149,7 +154,7 @@
     def _():
         pl.semaphore_wait(ready.at[1], 1)
 
-    for b in range(batches):
+    def others(b, carry):
         which = pl.ds(b * BATCH, BATCH)
         start(
             field.at[0, which, 1 + (rows_x - 1) * x_lo],
@@ -157,6 +162,9 @@
             across, 0, b,
         )
         send(0, b, (2, 3), 0)
+        return carry
+
+    lax.fori_loop(0, batches, others, 0)
     load_energy().wait()
     energy[...] = energy[...] - center_ref[0]
 
@@ -236,25 +244,33 @@
 
         lax.fori_loop(0, batches, batch, 0)
 
-    sent, done = [0], [0]
-
-    def send_more(count):
-        for _ in range(count):
-            if sent[0] < batches:
-                send(final, sent[0], (1, 3), 2)
-                sent[0] += 1
+    sent, done = [max(batches - lead, 0) for lead in LEAD], [0]
+
+    def send_more(of_core, count):
+        low = sent[of_core]
+        sent[of_core] = min(low + count, batches)
+        if sent[of_core] > low:
+
+            @pl.when(core == of_core)
+            def _():
+                def one(b, carry):
+                    send(final, b, (1, 3), 2)
+                    return carry
+
+                lax.fori_loop(low, sent[of_core], one, 0)
 
     def finish_more(count):
-        for _ in range(count):
-            if done[0] < sent[0]:
-                settled(done[0], 2, 2).wait_recv()
-
-                def one(q, carry, b=done[0]):
-                    last_high(b * BATCH + q)
-                    return carry
-
-                lax.fori_loop(0, BATCH, one, 0)
-                done[0] += 1
+        low = done[0]
+        done[0] = max(low, min(low + count, *sent))
+
+        def one(b, carry):
+            settled(b, 2, 2).wait_recv()
+            for q in range(BATCH):
+                last_high(b * BATCH + q)
+            return carry
+
+        if done[0] > low:
+            lax.fori_loop(low, done[0], one, 0)
 
     lane = lax.broadcasted_iota(jnp.int32, (probes, 128), 1)
 
@@ -266,17 +282,28 @@
 
     sums = column_sums(jnp.zeros((probes, 128), jnp.float32), range(2 * final))
 
-    for b in range(batches):
+    def low_half(b, carry):
         settled(b, 2, final % 2).wait_recv()
-
-        def one(q, carry, b=b):
+        for q in range(BATCH):
             last_low(b * BATCH + q)
-            return carry
-
-        lax.fori_loop(0, BATCH, one, 0)
-        if b >= LEAD:
-            send_more(1)
-
+        if LEAD[0] == LEAD[1]:
+
+            @pl.when(b >= LEAD[0])
+            def _():
+                send(final, b - LEAD[0], (1, 3), 2)
+        else:
+
+            @pl.when((b >= LEAD[0]) & (core == 0))
+            def _():
+                send(final, b - LEAD[0], (1, 3), 2)
+
+            @pl.when((b >= LEAD[1]) & (core == 1))
+            def _():
+                send(final, b - LEAD[1], (1, 3), 2)
+
+        return carry
+
+    lax.fori_loop(0, batches, low_half, 0)
     sums = column_sums(sums, range(2 * final, 2 * STEPS))
 
     for g, (peers, place) in enumerate(groups):
@@ -290,7 +317,8 @@
                 device_id={"gx": x, "gy": y},
                 device_id_type=MESH,
             ).start()
-        send_more(LATER[g])
+        for of_core in range(2):
+            send_more(of_core, LATER[of_core][g])
         finish_more(FINISH[g])
         whole = slots.at[g, pl.ds(0, len(peers))]
         arrived = pltpu.make_async_remote_copy(
@@ -309,10 +337,13 @@
     sums_ref[...] = sums
     finish_more(batches)
 
-    for b in range(batches):
+    def drain(b, carry):
         settled(b, 4, (final - 1) % 2).wait_send()
         settled(b, 2, final % 2).wait_send()
         settled(b, 2, 2).wait_send()
+        return carry
+
+    lax.fori_loop(0, batches, drain, 0)
 
 
 def finish(sites, last_ref, sums_ref, out_ref, moments_ref, sem):
@@ -353,7 +384,7 @@
                 pltpu.VMEM((STEPS, 2, n_probes, rows_x, rows_z), jnp.float32),
                 pltpu.VMEM((STEPS, 2, n_probes, rows_x, rows_z), jnp.float32),
                 pltpu.VMEM((2 * STEPS, n_probes, 8, 128), jnp.float32),
-                pltpu.VMEM((3, 8, n_probes, 128), jnp.float32),
+                pltpu.VMEM((2, 16, n_probes, 128), jnp.float32),
                 pltpu.SemaphoreType.DMA((n_probes + 1,)),
                 pltpu.SemaphoreType.DMA((3, n_probes // BATCH)),
                 pltpu.SemaphoreType.DMA((3, n_probes // BATCH)),

time: 84.3 us -> 82.4 us (0.977)
  Pallas kernels: 82.3 us -> 80.4 us
    pallas_call x1, Pallas kernels: 79.6 us -> 77.7 us  [local(): pl.pallas_call(functools.partial(kernel, counts), out_shape=(jax.ShapeDty...]
where the time goes in v5:
time: 82.4 us; the launch traced here: 82.3 us
  Pallas kernels  80.4 us (98%)
  between operations  1.93 us (2%)
    pallas_call x1, Pallas kernels, local(): pl.pallas_call(functools.partial(kernel, counts), out_shape=(jax.ShapeDty...  77.7 us
    pallas_call x1, Pallas kernels, local(): pl.pallas_call(functools.partial(finish, sites), out_shape=(jax.ShapeDtyp...  2.66 us

profile of v5, /device:TPU:1, one launch (start us, length us, event | category | flops | bytes accessed | tf_op | source)
XLA Modules:
  0.0 82.3 jit_solution(655312771853871486)
XLA Ops:
  1.9 77.7 %shard_map.59 = (f32[8,16,16,512]{3,2,1,0:T(8,128)S(1)}, f32[8,128]{1,0:T(8,128)S(1)}) custom-call(f32[1]{0:T(128)S(6)} %copy.6.center_ref, f32[1]{0:T(128)S(6)} %copy.7.width_ref, f32[8,16,16,512]{3,2,1,0:T(8,128)} %probes_ref.1, f32[16,16,512]{2,1,0:T(8,128)} %disorder_ref.1), custom_call_target="tpu_custom_call" | custom-call | tf_op jit(solution)/shard_map/pallas_call | solution.py:373
  79.6 2.7 %shard_map.60 = (f32[8,16,16,512]{3,2,1,0:T(8,128)}, f32[8,8]{1,0:T(8,128)}) custom-call(f32[8,16,16,512]{3,2,1,0:T(8,128)S(1)} %get-tuple-element.4.last_ref, f32[8,128]{1,0:T(8,128)S(1)} %get-tuple-element.5.sums_ref), custom_call_target="tpu_custom_call" | custom-call | tf_op jit(solution)/shard_map/pallas_call | solution.py:400

commit v6 on v5

--- a/solution.py
+++ b/solution.py
@@ -11,8 +11,8 @@
 BATCH = 1
 MESH = pl.DeviceIdType.MESH
 LEAD = (5, 2)
-ORDER = (0, 1, 2, 3)
-UNROLL = 8
+ORDER = (3, 2, 1, 0)
+UNROLL = 16
 LATER = ((8, 8), (8, 8))
 FINISH = (4, 8)
 VMEM_LIMIT = 48 * 1024 * 1024
@@ -239,7 +239,7 @@
             lax.fori_loop(0, BATCH, one, 0)
             if n > 0:
                 settled(b, 4, (n + 1) % 2).wait_send()
-            send(n + 1, b, ORDER if n + 1 < final else (0, 2), (n + 1) % 2)
+            send(n + 1, b, ORDER if n + 1 < final else (2, 0), (n + 1) % 2)
             return carry
 
         lax.fori_loop(0, batches, batch, 0)
@@ -254,7 +254,7 @@
             @pl.when(core == of_core)
             def _():
                 def one(b, carry):
-                    send(final, b, (1, 3), 2)
+                    send(final, b, (3, 1), 2)
                     return carry
 
                 lax.fori_loop(low, sent[of_core], one, 0)
@@ -290,16 +290,16 @@
 
             @pl.when(b >= LEAD[0])
             def _():
-                send(final, b - LEAD[0], (1, 3), 2)
+                send(final, b - LEAD[0], (3, 1), 2)
         else:
 
             @pl.when((b >= LEAD[0]) & (core == 0))
             def _():
-                send(final, b - LEAD[0], (1, 3), 2)
+                send(final, b - LEAD[0], (3, 1), 2)
 
             @pl.when((b >= LEAD[1]) & (core == 1))
             def _():
-                send(final, b - LEAD[1], (1, 3), 2)
+                send(final, b - LEAD[1], (3, 1), 2)
 
         return carry
 

time: 82.4 us -> 82.1 us (level)
  no operation moved by 1% of the time
where the time goes in v6:
time: 82.1 us; the launch traced here: 82 us
  Pallas kernels  80.1 us (98%)
  between operations  1.93 us (2%)
    pallas_call x1, Pallas kernels, local(): pl.pallas_call(functools.partial(kernel, counts), out_shape=(jax.ShapeDty...  77.4 us
    pallas_call x1, Pallas kernels, local(): pl.pallas_call(functools.partial(finish, sites), out_shape=(jax.ShapeDtyp...  2.66 us

profile of v6, /device:TPU:1, one launch (start us, length us, event | category | flops | bytes accessed | tf_op | source)
XLA Modules:
  0.0 82.0 jit_solution(5430465048225222508)
XLA Ops:
  1.9 77.4 %shard_map.59 = (f32[8,16,16,512]{3,2,1,0:T(8,128)S(1)}, f32[8,128]{1,0:T(8,128)S(1)}) custom-call(f32[1]{0:T(128)S(6)} %copy.6.center_ref, f32[1]{0:T(128)S(6)} %copy.7.width_ref, f32[8,16,16,512]{3,2,1,0:T(8,128)} %probes_ref.1, f32[16,16,512]{2,1,0:T(8,128)} %disorder_ref.1), custom_call_target="tpu_custom_call" | custom-call | tf_op jit(solution)/shard_map/pallas_call | solution.py:373
  79.4 2.7 %shard_map.60 = (f32[8,16,16,512]{3,2,1,0:T(8,128)}, f32[8,8]{1,0:T(8,128)}) custom-call(f32[8,16,16,512]{3,2,1,0:T(8,128)S(1)} %get-tuple-element.4.last_ref, f32[8,128]{1,0:T(8,128)S(1)} %get-tuple-element.5.sums_ref), custom_call_target="tpu_custom_call" | custom-call | tf_op jit(solution)/shard_map/pallas_call | solution.py:400

commit v7 on v6

--- a/solution.py
+++ b/solution.py
@@ -40,9 +40,13 @@
     def device(x, y, z, c):
         return (2 * z + lax.rem(x, 2), 4 * y + 2 * (x // 2) + c)
 
+    def hops(step):
+        x, y, z, c = step
+        return -(min(x, 4 - x) + min(y, wide_y - y) + min(z, wide_z - z))
+
     def group(pairs):
         return [device(lax.rem(chip_x + x, 4), lax.rem(chip_y + y, wide_y), lax.rem(chip_z + z, wide_z),
-                       lax.rem(core + c, 2)) for x, y, z, c in pairs]
+                       lax.rem(core + c, 2)) for x, y, z, c in sorted(pairs, key=hops)]
 
     group_x = group([(x, 0, 0, c) for x in range(4) for c in range(2) if x or c])
     group_yz = group([(0, y, z, 0) for y in range(wide_y) for z in range(wide_z) if y or z])

time: 82.1 us -> 82.1 us (level)
  no operation moved by 1% of the time
where the time goes in v7:
time: 82.1 us; the launch traced here: 81.9 us
  Pallas kernels  80 us (97%)
  between operations  1.93 us (2%)
    pallas_call x1, Pallas kernels, local(): pl.pallas_call(functools.partial(kernel, counts), out_shape=(jax.ShapeDty...  77.3 us
    pallas_call x1, Pallas kernels, local(): pl.pallas_call(functools.partial(finish, sites), out_shape=(jax.ShapeDtyp...  2.66 us

profile of v7, /device:TPU:1, one launch (start us, length us, event | category | flops | bytes accessed | tf_op | source)
XLA Modules:
  0.0 81.9 jit_solution(14790371396773030684)
XLA Ops:
  1.9 77.3 %shard_map.59 = (f32[8,16,16,512]{3,2,1,0:T(8,128)S(1)}, f32[8,128]{1,0:T(8,128)S(1)}) custom-call(f32[1]{0:T(128)S(6)} %copy.6.center_ref, f32[1]{0:T(128)S(6)} %copy.7.width_ref, f32[8,16,16,512]{3,2,1,0:T(8,128)} %probes_ref.1, f32[16,16,512]{2,1,0:T(8,128)} %disorder_ref.1), custom_call_target="tpu_custom_call" | custom-call | tf_op jit(solution)/shard_map/pallas_call | solution.py:377
  79.3 2.7 %shard_map.60 = (f32[8,16,16,512]{3,2,1,0:T(8,128)}, f32[8,8]{1,0:T(8,128)}) custom-call(f32[8,16,16,512]{3,2,1,0:T(8,128)S(1)} %get-tuple-element.4.last_ref, f32[8,128]{1,0:T(8,128)S(1)} %get-tuple-element.5.sums_ref), custom_call_target="tpu_custom_call" | custom-call | tf_op jit(solution)/shard_map/pallas_call | solution.py:404
